TPU v7x, 8 devices: a whole 2x2x1 slice. The times are simulated.
8 devices in a mesh: dp: 2 (over z, y), cp: 4 (over x, core).
Axes of the slice: x: 2, y: 2, z: 1, core: 2. Of those that a mesh axis runs over, the one named last changes fastest.
Arguments:
- x: bfloat16 [1024, 2048], P(('dp', 'cp')), parts along dimension 0
- k_cache: bfloat16 [32768, 8, 128], P(('dp', 'cp')), parts along dimension 0
- v_cache: bfloat16 [32768, 8, 128], P(('dp', 'cp')), parts along dimension 0
- ln_gain: bfloat16 [2048], replicated
- w_q: bfloat16 [2048, 2048], replicated
- w_k: bfloat16 [2048, 1024], replicated
- w_v: bfloat16 [2048, 1024], replicated
- w_o: bfloat16 [2048, 2048], replicated
- q_gain: bfloat16 [128], replicated
- k_gain: bfloat16 [128], replicated
Outputs:
- output 1: bfloat16 [1024, 2048], P(('dp', 'cp')), parts along dimension 0
- output 2: bfloat16 [1024, 8, 128], P(('dp', 'cp')), parts along dimension 0
- output 3: bfloat16 [1024, 8, 128], P(('dp', 'cp')), parts along dimension 0
There are 2 independent parts. A program takes and returns all parts, laid end to end along the dimension named above; an argument that names none is the same for every part.
All inputs are finite; a program needn't handle non-finite values.
Results may differ from a plain program's by a relative error of at most 0.0121848.
Values are sent between devices in bfloat16 or wider.
A program may use at most 1 GiB of HBM per device.

v0:
```python
import jax
import jax.numpy as jnp
from jax import lax
from jax.sharding import PartitionSpec as P

HEAD_DIM = 128
ROPE_THETA = 1.0e6
NORM_EPS = 1.0e-6
MASK_VALUE = -1.0e30


def rms_norm(vals, gain):
    mean_sq = jnp.mean(vals * vals, axis=-1, keepdims=True)
    return vals * lax.rsqrt(mean_sq + NORM_EPS) * gain


def apply_rope(vals, positions):
    half = HEAD_DIM // 2
    inv_freq = ROPE_THETA ** (-jnp.arange(half, dtype=jnp.float32) * (2.0 / HEAD_DIM))
    angles = positions.astype(jnp.float32)[:, None] * inv_freq[None, :]
    cos_tab = jnp.cos(angles)[:, None, :]
    sin_tab = jnp.sin(angles)[:, None, :]
    first = vals[..., :half]
    second = vals[..., half:]
    return jnp.concatenate([first * cos_tab - second * sin_tab, second * cos_tab + first * sin_tab], axis=-1)


def project_rows(x_wide, ln_gain, w_q, w_k, w_v, q_gain, k_gain, positions):
    rows = x_wide.shape[0]
    hidden = rms_norm(x_wide, ln_gain.astype(jnp.float32)).astype(jnp.bfloat16)
    q_raw = jnp.dot(hidden, w_q, preferred_element_type=jnp.float32).astype(jnp.bfloat16).reshape(rows, -1, HEAD_DIM)
    k_raw = jnp.dot(hidden, w_k, preferred_element_type=jnp.float32).astype(jnp.bfloat16).reshape(rows, -1, HEAD_DIM)
    v_new = jnp.dot(hidden, w_v, preferred_element_type=jnp.float32).astype(jnp.bfloat16).reshape(rows, -1, HEAD_DIM)
    q_rot = apply_rope(rms_norm(q_raw.astype(jnp.float32), q_gain.astype(jnp.float32)), positions).astype(jnp.bfloat16)
    k_new = apply_rope(rms_norm(k_raw.astype(jnp.float32), k_gain.astype(jnp.float32)), positions).astype(jnp.bfloat16)
    return q_rot, k_new, v_new


def partial_attend(q_grp, keys, vals, allowed):
    scale = HEAD_DIM ** -0.5
    scores = jnp.einsum('rkgd,skd->krgs', q_grp, keys, preferred_element_type=jnp.float32) * scale
    if allowed is not None:
        scores = jnp.where(allowed[None, :, None, :], scores, MASK_VALUE)
    peak = jnp.max(scores, axis=-1)
    weights = jnp.exp(scores - peak[..., None])
    weighted = jnp.einsum('krgs,skd->krgd', weights.astype(jnp.bfloat16), vals, preferred_element_type=jnp.float32)
    return peak, jnp.sum(weights, axis=-1), weighted


def combine_two(first, second):
    peak_a, sum_a, acc_a = first
    peak_b, sum_b, acc_b = second
    top_peak = jnp.maximum(jnp.max(peak_a, axis=0), jnp.max(peak_b, axis=0))
    factor_a = jnp.exp(peak_a - top_peak[None])
    factor_b = jnp.exp(peak_b - top_peak[None])
    total_sum = jnp.sum(factor_a * sum_a, axis=0) + jnp.sum(factor_b * sum_b, axis=0)
    total = jnp.sum(factor_a[..., None] * acc_a, axis=0) + jnp.sum(factor_b[..., None] * acc_b, axis=0)
    return total / total_sum[..., None]


def solution(mesh):
    cp_size = mesh.shape['cp']
    row_spec = P(('dp', 'cp'), None)
    cache_spec = P(('dp', 'cp'), None, None)
    whole = P()

    def device_step(x_rows, k_cache, v_cache, ln_gain, w_q, w_k, w_v, w_o, q_gain, k_gain):
        rows = x_rows.shape[0]
        prefix_len = k_cache.shape[0] * cp_size
        kv_heads = k_cache.shape[1]
        q_heads = w_q.shape[1] // HEAD_DIM
        group = q_heads // kv_heads
        my_index = lax.axis_index('cp')
        row_ids = my_index * rows + jnp.arange(rows)
        key_ids = jnp.arange(rows)
        x_wide = x_rows.astype(jnp.float32)
        q_rot, k_new, v_new = project_rows(x_wide, ln_gain, w_q, w_k, w_v, q_gain, k_gain, prefix_len + row_ids)
        q_grp = q_rot.reshape(rows, kv_heads, group, HEAD_DIM)
        every_q = lax.all_gather(q_grp, 'cp')
        every_k = lax.all_gather(k_new, 'cp')
        every_v = lax.all_gather(v_new, 'cp')

        def block_work(block):
            q_block, k_block, v_block, source = block
            prefix_part = partial_attend(q_block, k_cache, v_cache, None)
            allowed = (source * rows + key_ids)[None, :] <= row_ids[:, None]
            new_part = partial_attend(q_grp, k_block, v_block, allowed)
            return prefix_part, new_part

        prefix_parts, new_parts = lax.map(block_work, (every_q, every_k, every_v, jnp.arange(cp_size)))
        returned = tuple(lax.all_to_all(piece, 'cp', 0, 0, tiled=True) for piece in prefix_parts)
        attended = combine_two(returned, new_parts)
        attended = jnp.transpose(attended, (1, 0, 2, 3)).reshape(rows, q_heads * HEAD_DIM).astype(jnp.bfloat16)
        out = (x_wide + jnp.dot(attended, w_o, preferred_element_type=jnp.float32)).astype(jnp.bfloat16)
        return out, k_new, v_new

    return jax.shard_map(device_step, mesh=mesh, in_specs=(row_spec, cache_spec, cache_spec, whole, whole, whole, whole, whole, whole, whole), out_specs=(row_spec, cache_spec, cache_spec), check_vma=False)
```

profile of v0, /device:TPU:0, one launch (start us, length us, event | category | flops | bytes accessed | tf_op | source)
XLA Modules:
  0.0 364.0 jit_solution(5662049967756462038)
XLA Ops:
  9.1 3.2 fusion.36
  14.2 3.1 fusion.35
  20.1 4.7 %fusion.33 = f32[16,8,16,128]{3,1,2,0:T(8,128)S(1)} fusion(bf16[2048,2048]{1,0:T(8,128)(2,1)} %param.16, bf16[128,2048]{1,0:T(8,128)(2,1)S(1)} %copy-done, f32[2048]{0:T(1024)S(1)} %convert_element_type.77, f32[128]{0:T(128)S(1)} %add_rsqrt_fusion.2), kind=kOutput, calls=%fused_computation.45 | convolution fusion | flops 1075314688 | bytes 9970176 | tf_op jit(solution)/shard_map/dot_general | solution.py:31
  28.2 7.7 %copy.93 = bf16[4096,8,128]{2,0,1:T(8,128)(2,1)} copy(bf16[4096,8,128]{2,1,0:T(8,128)(2,1)} %param.13) | data formatting | bytes 16777216
  35.8 7.7 %copy.94 = bf16[4096,8,128]{2,0,1:T(8,128)(2,1)} copy(bf16[4096,8,128]{2,1,0:T(8,128)(2,1)} %param.14) | data formatting | bytes 16777216
  45.7 21.7 %all-gather.4.cloned.1.call-done = bf16[4,128,8,2,128]{4,2,3,1,0:T(8,128)(2,1)} async-done(((bf16[1,128,8,2,128]{4,2,3,1,0:T(8,128)(2,1)}), bf16[4,128,8,2,128]{4,2,3,1,0:T(8,128)(2,1)}) %all-gather.4.cloned.1.call-update) | async-done | bytes 2097168 | tf_op jit(solution)/shard_map/all_gather | solution.py:79
  67.3 215.6 %while.21 = (s32[]{:T(128)}, f32[4,8,128,2]{2,3,1,0:T(2,128)S(1)}, f32[4,8,128,2]{2,3,1,0:T(2,128)S(1)}, f32[4,8,128,2,128]{4,2,3,1,0:T(8,128)}, f32[4,8,128,2]{...) while((s32[]{:T(128)}, f32[4,8,128,2]{2,3,1,0:T(2,128)S(1)}, ...), condition=%wide.region_8.9_spmd.clone, body=%wide.region_3.8_spmd.clone.sunk | while | flops 4498137088 | bytes 126519504 | solution.py:90
  73.6 16.5 %multiply_reduce_fusion.8 = (f32[8,128,2]{1,2,0:T(2,128)S(1)}, f32[8,128,2,4096]{3,1,2,0:T(8,128)}) fusion(bf16[4096,8,128]{2,0,1:T(8,128)(2,1)} %get-tuple-element.434, bf16[1,128,8,2,128]{4,2,3,1,0:T(8,128)(2,1)S(1)} %constant_dynamic-slice_fusion.6), kind=kOutput, calls=%fused_computation.3.clone.1 | convolution fusion | flops 2164258816 | bytes 42475520 | tf_op jit(solution)/shard_map/while/body/eval_jaxpr/rkgd,skd->krgs/dot_general | solution.py:41
  90.1 14.0 %fusion.64 = f32[8,128,2]{1,2,0:T(2,128)S(1)} fusion(f32[8,128,2,4096]{3,1,2,0:T(8,128)} %get-tuple-element.384, f32[8,128,2]{1,2,0:T(2,128)S(1)} %get-tuple-element.385), kind=kLoop, calls=%fused_computation.5.clone.1 | loop fusion | flops 25163776 | bytes 33570816 | tf_op jit(solution)/shard_map/while/body/eval_jaxpr/reduce_sum | solution.py:47
  104.1 17.1 %fusion.65 = f32[4,8,128,2,128]{4,2,3,1,0:T(8,128)} fusion(f32[4,8,128,2,128]{4,2,3,1,0:T(8,128)} %get-tuple-element.412, s32[]{:T(128)S(6)} %copy.139, bf16[4096,8,128]{2,0,1:T(8,128)(2,1)} %get-tuple-element.435, f32[8,128,2,4096]{3,1,2,0:T(8,128)} %get-tuple-element.384, f32[8,128,2]{1,2,0:T(2,128)S(1)} %get-tuple-element.385), kind=kOutput, calls=%fused_computation.13.clone.1 | convolution fusion | flops 2172649472 | bytes 42999812 | tf_op jit(solution)/shard_map/while/body/eval_jaxpr/krgs,skd->krgd/dot_general | solution.py:46
  127.5 16.5 %multiply_reduce_fusion.8 = (f32[8,128,2]{1,2,0:T(2,128)S(1)}, f32[8,128,2,4096]{3,1,2,0:T(8,128)}) fusion(bf16[4096,8,128]{2,0,1:T(8,128)(2,1)} %get-tuple-element.434, bf16[1,128,8,2,128]{4,2,3,1,0:T(8,128)(2,1)S(1)} %constant_dynamic-slice_fusion.6), kind=kOutput, calls=%fused_computation.3.clone.1 | convolution fusion | flops 2164258816 | bytes 42475520 | tf_op jit(solution)/shard_map/while/body/eval_jaxpr/rkgd,skd->krgs/dot_general | solution.py:41
  144.0 14.0 %fusion.64 = f32[8,128,2]{1,2,0:T(2,128)S(1)} fusion(f32[8,128,2,4096]{3,1,2,0:T(8,128)} %get-tuple-element.384, f32[8,128,2]{1,2,0:T(2,128)S(1)} %get-tuple-element.385), kind=kLoop, calls=%fused_computation.5.clone.1 | loop fusion | flops 25163776 | bytes 33570816 | tf_op jit(solution)/shard_map/while/body/eval_jaxpr/reduce_sum | solution.py:47
  158.0 17.1 %fusion.65 = f32[4,8,128,2,128]{4,2,3,1,0:T(8,128)} fusion(f32[4,8,128,2,128]{4,2,3,1,0:T(8,128)} %get-tuple-element.412, s32[]{:T(128)S(6)} %copy.139, bf16[4096,8,128]{2,0,1:T(8,128)(2,1)} %get-tuple-element.435, f32[8,128,2,4096]{3,1,2,0:T(8,128)} %get-tuple-element.384, f32[8,128,2]{1,2,0:T(2,128)S(1)} %get-tuple-element.385), kind=kOutput, calls=%fused_computation.13.clone.1 | convolution fusion | flops 2172649472 | bytes 42999812 | tf_op jit(solution)/shard_map/while/body/eval_jaxpr/krgs,skd->krgd/dot_general | solution.py:46
  181.4 16.5 %multiply_reduce_fusion.8 = (f32[8,128,2]{1,2,0:T(2,128)S(1)}, f32[8,128,2,4096]{3,1,2,0:T(8,128)}) fusion(bf16[4096,8,128]{2,0,1:T(8,128)(2,1)} %get-tuple-element.434, bf16[1,128,8,2,128]{4,2,3,1,0:T(8,128)(2,1)S(1)} %constant_dynamic-slice_fusion.6), kind=kOutput, calls=%fused_computation.3.clone.1 | convolution fusion | flops 2164258816 | bytes 42475520 | tf_op jit(solution)/shard_map/while/body/eval_jaxpr/rkgd,skd->krgs/dot_general | solution.py:41
  197.9 14.0 %fusion.64 = f32[8,128,2]{1,2,0:T(2,128)S(1)} fusion(f32[8,128,2,4096]{3,1,2,0:T(8,128)} %get-tuple-element.384, f32[8,128,2]{1,2,0:T(2,128)S(1)} %get-tuple-element.385), kind=kLoop, calls=%fused_computation.5.clone.1 | loop fusion | flops 25163776 | bytes 33570816 | tf_op jit(solution)/shard_map/while/body/eval_jaxpr/reduce_sum | solution.py:47
  211.9 17.1 %fusion.65 = f32[4,8,128,2,128]{4,2,3,1,0:T(8,128)} fusion(f32[4,8,128,2,128]{4,2,3,1,0:T(8,128)} %get-tuple-element.412, s32[]{:T(128)S(6)} %copy.139, bf16[4096,8,128]{2,0,1:T(8,128)(2,1)} %get-tuple-element.435, f32[8,128,2,4096]{3,1,2,0:T(8,128)} %get-tuple-element.384, f32[8,128,2]{1,2,0:T(2,128)S(1)} %get-tuple-element.385), kind=kOutput, calls=%fused_computation.13.clone.1 | convolution fusion | flops 2172649472 | bytes 42999812 | tf_op jit(solution)/shard_map/while/body/eval_jaxpr/krgs,skd->krgd/dot_general | solution.py:46
  235.3 16.5 %multiply_reduce_fusion.8 = (f32[8,128,2]{1,2,0:T(2,128)S(1)}, f32[8,128,2,4096]{3,1,2,0:T(8,128)}) fusion(bf16[4096,8,128]{2,0,1:T(8,128)(2,1)} %get-tuple-element.434, bf16[1,128,8,2,128]{4,2,3,1,0:T(8,128)(2,1)S(1)} %constant_dynamic-slice_fusion.6), kind=kOutput, calls=%fused_computation.3.clone.1 | convolution fusion | flops 2164258816 | bytes 42475520 | tf_op jit(solution)/shard_map/while/body/eval_jaxpr/rkgd,skd->krgs/dot_general | solution.py:41
  251.8 14.0 %fusion.64 = f32[8,128,2]{1,2,0:T(2,128)S(1)} fusion(f32[8,128,2,4096]{3,1,2,0:T(8,128)} %get-tuple-element.384, f32[8,128,2]{1,2,0:T(2,128)S(1)} %get-tuple-element.385), kind=kLoop, calls=%fused_computation.5.clone.1 | loop fusion | flops 25163776 | bytes 33570816 | tf_op jit(solution)/shard_map/while/body/eval_jaxpr/reduce_sum | solution.py:47
  265.8 17.1 %fusion.65 = f32[4,8,128,2,128]{4,2,3,1,0:T(8,128)} fusion(f32[4,8,128,2,128]{4,2,3,1,0:T(8,128)} %get-tuple-element.412, s32[]{:T(128)S(6)} %copy.139, bf16[4096,8,128]{2,0,1:T(8,128)(2,1)} %get-tuple-element.435, f32[8,128,2,4096]{3,1,2,0:T(8,128)} %get-tuple-element.384, f32[8,128,2]{1,2,0:T(2,128)S(1)} %get-tuple-element.385), kind=kOutput, calls=%fused_computation.13.clone.1 | convolution fusion | flops 2172649472 | bytes 42999812 | tf_op jit(solution)/shard_map/while/body/eval_jaxpr/krgs,skd->krgd/dot_general | solution.py:46
  283.0 6.4 %all_to_all.15 = f32[4,8,128,2]{2,3,1,0:T(2,128)S(1)} all-to-all(f32[4,8,128,2]{2,3,1,0:T(2,128)S(1)} %get-tuple-element.90), channel_id=1, replica_groups=mesh['dp'=2,'cp'=4] {'cp'}, dimensions={0} | all-to-all | bytes 65536 | tf_op jit(solution)/shard_map/all_to_all | solution.py:91
  289.4 6.3 %all_to_all.16 = f32[4,8,128,2]{2,3,1,0:T(2,128)S(1)} all-to-all(f32[4,8,128,2]{2,3,1,0:T(2,128)S(1)} %get-tuple-element.94), channel_id=1, replica_groups=mesh['dp'=2,'cp'=4] {'cp'}, dimensions={0} | all-to-all | bytes 65536 | tf_op jit(solution)/shard_map/all_to_all | solution.py:91
  295.7 4.9 %all-to-all-start.1 = ((f32[4,8,128,2,128]{4,2,3,1,0:T(8,128)}), f32[4,8,128,2,128]{4,2,3,1,0:T(8,128)}, u32[]{:S(2)}, u32[]{:S(2)}) async-start(f32[4,8,128,2,128]{4,2,3,1,0:T(8,128)} %get-tuple-element.92), calls=%async_computation.1 | async-start | bytes 8388608 | tf_op jit(solution)/shard_map/all_to_all | solution.py:91
  304.5 43.9 %all-to-all-done.1 = f32[4,8,128,2,128]{4,2,3,1,0:T(8,128)} async-done(((f32[4,8,128,2,128]{4,2,3,1,0:T(8,128)}), f32[4,8,128,2,128]{4,2,3,1,0:T(8,128)}, u32[]{:S(2)}, u32[]{:S(2)}) %all-to-all-start.1) | async-done | bytes 4194336 | tf_op jit(solution)/shard_map/all_to_all | solution.py:91
  352.0 5.5 %fusion.32 = bf16[128,2048]{1,0:T(8,128)(2,1)} fusion(bf16[128,2048]{0,1:T(8,128)(2,1)S(1)} %bitcast.113, bf16[2048,2048]{1,0:T(8,128)(2,1)} %param.19, bf16[128,2048]{1,0:T(8,128)(2,1)S(1)} %copy-done.1), kind=kOutput, calls=%fused_computation.42 | convolution fusion | flops 1074528256 | bytes 9961472 | tf_op jit(solution)/shard_map/dot_general | solution.py:94
  (118 shorter events, 41.7 us)
Async XLA Ops:
  7.2 36.6 %all-gather.8.cloned.1.call-start = ((), (), s32[]{:S(2)}) async-start(), calls=%async_computation.5 | async-start | bytes 1310720 | tf_op jit(solution)/shard_map/all_gather | solution.py:81
  9.1 11.0 %copy-start.6 = (bf16[128]{0:T(256)(128)(2,1)S(1)}, bf16[128]{0:T(256)(128)(2,1)}, u32[]{:S(2)}) copy-start(bf16[128]{0:T(256)(128)(2,1)} %param.20) | copy-start | bytes 772
  9.1 11.0 %copy-start = (bf16[128,2048]{1,0:T(8,128)(2,1)S(1)}, bf16[128,2048]{1,0:T(8,128)(2,1)}, u32[]{:S(2)}) copy-start(bf16[128,2048]{1,0:T(8,128)(2,1)} %param.12) | copy-start | bytes 1572868
  13.1 32.6 %all-gather.6.cloned.1.call-start = ((), (), s32[]{:S(2)}) async-start(), calls=%async_computation.4 | async-start | bytes 1310720 | tf_op jit(solution)/shard_map/all_gather | solution.py:80
  18.4 0.7 copy-start.2
  18.4 0.8 copy-start.4
  20.0 47.3 %all-gather.4.cloned.1.call-start = ((), (), s32[]{:S(2)}) async-start(), calls=%async_computation.3 | async-start | bytes 2621440 | tf_op jit(solution)/shard_map/all_gather | solution.py:79
  283.0 17.6 %copy-start.3 = (bf16[128,8,64]{2,1,0:T(8,128)(2,1)S(1)}, bf16[128,8,64]{2,1,0:T(8,128)(2,1)}, u32[]{:S(2)}) copy-start(bf16[128,8,64]{2,1,0:T(8,128)(2,1)} %copy-done.2) | copy-start | bytes 393220
  283.0 17.6 %copy-start.5 = (bf16[128,8,64]{2,1,0:T(8,128)(2,1)S(1)}, bf16[128,8,64]{2,1,0:T(8,128)(2,1)}, u32[]{:S(2)}) copy-start(bf16[128,8,64]{2,1,0:T(8,128)(2,1)} %copy-done.4) | copy-start | bytes 393220
  295.7 52.7 %all-to-all-start.1 = ((f32[4,8,128,2,128]{4,2,3,1,0:T(8,128)}), f32[4,8,128,2,128]{4,2,3,1,0:T(8,128)}, u32[]{:S(2)}, u32[]{:S(2)}) async-start(f32[4,8,128,2,128]{4,2,3,1,0:T(8,128)} %get-tuple-element.92), calls=%async_computation.1 | async-start | bytes 8388608 | tf_op jit(solution)/shard_map/all_to_all | solution.py:91
  300.6 51.5 %copy-start.1 = (bf16[128,2048]{1,0:T(8,128)(2,1)S(1)}, bf16[128,2048]{1,0:T(8,128)(2,1)}, u32[]{:S(2)}) copy-start(bf16[128,2048]{1,0:T(8,128)(2,1)} %param.12) | copy-start | bytes 1572868
Sparse Core Ops, SparseCore 0:
  13.2 16.5 all-gather.7
  31.9 13.7 all-gather.5
  47.8 19.5 all-gather.3
where the time goes:
time: 366 us; the launch traced here: 364 us
  matrix products  158 us (43%)
  other arithmetic  69.8 us (19%)
  waiting for transfers between devices  67.5 us (18%)
  local copies, waits for them, and re-layouts  34.5 us (9%)
  between operations  14.1 us (4%)
  blocking collectives  12.7 us (3%)
  starting transfers between devices  4.98 us (1%)
    dot_general x8, matrix products, partial_attend(): jnp.einsum('krgs,skd->krgd', weights.astype(jnp.bfloat16), vals, preferre...  73.8 us
    dot_general x8, matrix products, partial_attend(): jnp.einsum('rkgd,skd->krgs', q_grp, keys, preferred_element_type=jnp.floa...  67.4 us
    reduce_sum x8, other arithmetic, partial_attend(): return (peak, jnp.sum(weights, axis=-1), weighted)  56.7 us
    all_to_all x1, waiting for transfers between devices, device_step(): lax.all_to_all(piece, 'cp', 0, 0, tiled=True)  43.9 us
    all_gather x1, waiting for transfers between devices, device_step(): every_q = lax.all_gather(q_grp, 'cp')  21.7 us
    unnamed x19, local copies, waits for them, and re-layouts  17.1 us
    dynamic_slice x16, local copies, waits for them, and re-layouts, device_step(): lax.map(block_work, (every_q, every_k, every_v, jnp.arange(cp_size)))  14.5 us
    all_to_all x2, blocking collectives, device_step(): lax.all_to_all(piece, 'cp', 0, 0, tiled=True)  12.7 us
  transfers between devices with their start and end apart: 4, of which 3 were waited for; matrix products, arithmetic and copies ran while one was open for 9% of the time, Pallas kernels for 0%

commit v1 on v0

v1 whole, which is shorter than its diff:
```python
import functools
import math

import jax
import jax.numpy as jnp
from jax import lax
from jax.experimental import pallas as pl
from jax.experimental.pallas import tpu as pltpu
from jax.sharding import PartitionSpec as P

HEAD_DIM = 128
ROPE_THETA = 1.0e6
NORM_EPS = 1.0e-6
SCALE_LOG2 = HEAD_DIM ** -0.5 * math.log2(math.e)
F32, BF16 = jnp.float32, jnp.bfloat16
MESH = pl.DeviceIdType.MESH

KEY_TILE = 256
PREP = 256
GROUP = 8
LEAD = 3


def rms_norm(vals, gain):
    mean_sq = jnp.mean(vals * vals, axis=-1, keepdims=True)
    return vals * lax.rsqrt(mean_sq + NORM_EPS) * gain


def apply_rope(vals, positions):
    half = HEAD_DIM // 2
    inv_freq = ROPE_THETA ** (-jnp.arange(half, dtype=F32) * (2.0 / HEAD_DIM))
    angles = positions.astype(F32)[:, None] * inv_freq[None, :]
    cos_tab = jnp.cos(angles)[:, None, :]
    sin_tab = jnp.sin(angles)[:, None, :]
    first = vals[..., :half]
    second = vals[..., half:]
    return jnp.concatenate([first * cos_tab - second * sin_tab, second * cos_tab + first * sin_tab], axis=-1)


def project_rows(x_wide, ln_gain, w_q, w_k, w_v, q_gain, k_gain, positions):
    rows = x_wide.shape[0]
    hidden = rms_norm(x_wide, ln_gain.astype(F32)).astype(BF16)
    q_raw = jnp.dot(hidden, w_q, preferred_element_type=F32).astype(BF16).reshape(rows, -1, HEAD_DIM)
    k_raw = jnp.dot(hidden, w_k, preferred_element_type=F32).astype(BF16).reshape(rows, -1, HEAD_DIM)
    v_new = jnp.dot(hidden, w_v, preferred_element_type=F32).astype(BF16).reshape(rows, -1, HEAD_DIM)
    q_rot = apply_rope(rms_norm(q_raw.astype(F32), q_gain.astype(F32)), positions).astype(BF16)
    k_new = apply_rope(rms_norm(k_raw.astype(F32), k_gain.astype(F32)), positions).astype(BF16)
    return q_rot, k_new, v_new


def attend_kernel(n_keys, heads, q_own, k_new, v_new, k_hbm, v_hbm, att_ref,
                  kh, vt, sA, sB, sN, mbuf, lbuf, mcb, obuf, q_recv, part, sib_recv, comb, mir_recv, raw, wide,
                  copy_sem, q_send, q_sem, sib_send, sib_sem, mir_send, mir_sem):
    SB = (sA, sB)
    me = lax.axis_index("cp")
    sibling = me + 1 - 2 * lax.rem(me, 2)
    mirror = lax.rem(me + 2, 4)
    rows = 128
    tiles = n_keys // KEY_TILE
    units = 2 * heads
    TS = lambda t: slice(t * 256, (t + 1) * 256)

    def remote(src, dst, send, recv, to):
        return pltpu.make_async_remote_copy(src_ref=src, dst_ref=dst, send_sem=send, recv_sem=recv,
                                            device_id={"cp": to}, device_id_type=MESH)

    def cache_copy(i, which, slot):
        src = (k_hbm, v_hbm)[which]
        n = PREP * heads
        return pltpu.make_async_copy(src.at[pl.ds(pl.multiple_of(i * n, n), n), :], raw.at[which, slot], copy_sem.at[which, slot])

    for s in range(2):
        cache_copy(s, 0, s).start()
        cache_copy(s, 1, s).start()

    barrier = pltpu.get_barrier_semaphore()
    for peer in (sibling, mirror):
        pl.semaphore_signal(barrier, inc=1, device_id={"cp": peer}, device_id_type=MESH)
    pl.semaphore_wait(barrier, 2)

    def q_to_sibling(g):
        return remote(q_own.at[g], q_recv.at[0, g], q_send.at[0, g], q_sem.at[0, g], sibling)
    def q_to_mirror(g):
        return remote(q_own.at[g], q_recv.at[1, g], q_send.at[1, g], q_sem.at[1, g], mirror)
    def q_forward(g):
        return remote(q_recv.at[1, g], q_recv.at[2, g], q_send.at[2, g], q_sem.at[2, g], sibling)
    for g in range(heads):
        q_to_mirror(g).start()
    for g in range(heads):
        q_to_sibling(g).start()

    def prep(i, _):
        slot = lax.rem(i, 2)
        row = pl.ds(pl.multiple_of(i * PREP, PREP), PREP)
        cache_copy(i, 0, slot).wait()
        wide[0] = raw[0, slot].astype(F32)
        for h in range(heads):
            kh[h, row, :] = wide[0, pl.ds(h, PREP, stride=heads), :].astype(BF16)
        cache_copy(i, 1, slot).wait()
        wide[1] = raw[1, slot].astype(F32)
        for h in range(heads):
            vt[h, :, row] = wide[1, pl.ds(h, PREP, stride=heads), :].T.astype(BF16)
        @pl.when(i + 2 < n_keys // PREP)
        def _():
            cache_copy(i + 2, 0, slot).start()
            cache_copy(i + 2, 1, slot).start()
        return 0
    lax.fori_loop(0, n_keys // PREP, prep, 0)

    for g in range(heads):
        q_to_mirror(g).wait_recv()
        q_forward(g).start()
    for g in range(heads):
        q_to_sibling(g).wait_recv()
        q_forward(g).wait_recv()

    def sib_copy(kind, g):
        return remote(part.at[kind, g, 1], sib_recv.at[kind, g], sib_send.at[kind, g], sib_sem.at[kind, g], sibling)
    def mir_copy(g):
        return remote(comb.at[g], mir_recv.at[g], mir_send.at[g], mir_sem.at[g], mirror)

    def main_body():
        def q_cols(kind, g):
            if kind == 0:
                return jnp.concatenate([q_recv[1, g], q_recv[2, g]], axis=1)
            return jnp.concatenate([q_own[g], q_recv[0, g]], axis=1)

        def dot(a, b):
            return lax.dot_general(a, b, (((1,), (0,)), ((), ())), preferred_element_type=F32)

        def col_max(mx, s):
            return jnp.maximum(mx, jnp.max(s.reshape(s.shape[0] // 8, 8, 512), axis=0))

        def qk(q, g, kc, slot, mx):
            s = dot(kh[g, pl.ds(pl.multiple_of(kc * KEY_TILE, KEY_TILE), KEY_TILE), :], q)
            SB[slot][kc] = s
            return col_max(mx, s)

        def qk_new(q, kind, g, slot, mx):
            own, other = (me, sibling) if kind == 1 else (mirror, lax.rem(sibling + 2, 4))
            key = lax.broadcasted_iota(jnp.int32, (rows, 512), 0) + me * rows
            col = lax.broadcasted_iota(jnp.int32, (rows, 512), 1)
            row = lax.rem(col, rows) + jnp.where(col < 256, own, other) * rows
            s = jnp.where(key <= row, dot(k_new[g], q), -jnp.inf)
            sN[slot] = s
            return col_max(mx, s)

        def weights(s, mc, ls):
            p = jnp.exp2(s * SCALE_LOG2 - mc)
            return p.astype(BF16), ls + jnp.sum(p.reshape(s.shape[0] // 8, 8, 512), axis=0)

        def block(last, kind_n, g_n, g, b, par):
            steps = [("Q", i) for i in range(GROUP)] + [("Q", None)] * last
            for i in range(GROUP):
                steps.insert(LEAD + 2 * i, ("P", i))
            steps += [("P", None)] * last
            mx, ls, mc = mbuf[...], lbuf[...], mcb[0:1, :]
            q = q_cols(kind_n, g_n)
            acc = None
            for op, i in steps:
                if op == "Q" and i is None:
                    mx = qk_new(q, kind_n, g_n, 1 - par, mx)
                elif op == "Q":
                    mx = qk(q, g_n, b * GROUP + i, 1 - par, mx)
                else:
                    if i is None:
                        p, ls = weights(sN[par], mc, ls)
                        v = v_new[g]
                    else:
                        kc = b * GROUP + i
                        p, ls = weights(SB[par][kc], mc, ls)
                        v = vt[g, :, pl.ds(pl.multiple_of(kc * KEY_TILE, KEY_TILE), KEY_TILE)]
                    pv = dot(v, p)
                    acc = pv if acc is None else acc + pv
            mbuf[...] = mx
            lbuf[...] = ls
            if not last:
                obuf[...] += acc
                return None
            return obuf[...] + acc

        def merge(a, b):
            ma, mb = a[128:129, :], b[128:129, :]
            m = jnp.maximum(ma, mb)
            fa, fb = jnp.exp2(ma - m), jnp.exp2(mb - m)
            return a[0:128, :] * fa + b[0:128, :] * fb, m, a[129:130, :] * fa + b[129:130, :] * fb

        def unit(g, kind):
            par = kind
            if kind == 0:
                kind_n, g_n = 1, g
            else:
                kind_n, g_n = 0, jnp.minimum(g + 1, heads - 1)
            mcb[0:1, :] = jnp.max(mbuf[...], axis=0, keepdims=True) * SCALE_LOG2
            mbuf[...] = jnp.full(mbuf.shape, -jnp.inf, F32)
            lbuf[...] = jnp.zeros(lbuf.shape, F32)
            obuf[...] = jnp.zeros(obuf.shape, F32)
            nb = tiles // GROUP
            def ib(b, _):
                block(False, kind_n, g_n, g, b, par)
                return 0
            lax.fori_loop(0, nb - 1, ib, 0)
            acc = block(True, kind_n, g_n, g, nb - 1, par)
            for t in range(2):
                part[kind, g, t, 0:128, :] = acc[:, TS(t)]
                part[kind, g, t, 128:129, :] = mcb[0:1, TS(t)]
                part[kind, g, t, 129:130, :] = jnp.sum(lbuf[:, TS(t)], axis=0, keepdims=True)
            sib_copy(kind, g).start()
            if kind == 1:
                sib_copy(0, g).wait_recv()
                acc, m, total = merge(part.at[0, g, 0], sib_recv.at[0, g])
                comb[g, 0:128, :] = acc
                comb[g, 128:129, :] = m
                comb[g, 129:130, :] = total
                mir_copy(g).start()

        mbuf[...] = jnp.full(mbuf.shape, -jnp.inf, F32)
        q0 = q_cols(0, 0)
        def first(kc, _):
            mbuf[...] = qk(q0, 0, kc, 0, mbuf[...])
            return 0
        lax.fori_loop(0, tiles, first, 0)
        mbuf[...] = qk_new(q0, 0, 0, 0, mbuf[...])

        def body(g, _):
            unit(g, 0)
            unit(g, 1)
            return 0
        lax.fori_loop(0, heads, body, 0)

        def final(g, _):
            sib_copy(1, g).wait_recv()
            mir_copy(g).wait_recv()
            acc, m, total = merge(part.at[1, g, 0], sib_recv.at[1, g])
            mb = mir_recv[g, 128:129, :]
            top = jnp.maximum(m, mb)
            fa, fb = jnp.exp2(m - top), jnp.exp2(mb - top)
            acc = acc * fa + mir_recv[g, 0:128, :] * fb
            total = total * fa + mir_recv[g, 129:130, :] * fb
            o = acc / total
            for j in range(2):
                cols = pl.ds(pl.multiple_of((2 * g + j) * 128, 128), 128)
                att_ref[:, cols] = o[:, j * 128:(j + 1) * 128].T.astype(BF16)
            return 0
        lax.fori_loop(0, heads, final, 0)

    main_body()

    def drain(g, _):
        q_to_mirror(g).wait_send()
        q_to_sibling(g).wait_send()
        q_forward(g).wait_send()
        sib_copy(0, g).wait_send()
        sib_copy(1, g).wait_send()
        mir_copy(g).wait_send()
        return 0
    lax.fori_loop(0, heads, drain, 0)


def attend(q_own, k_new, v_new, k_cache, v_cache):
    n_keys, heads, _ = k_cache.shape
    rows = q_own.shape[2] // 2
    vm = pl.BlockSpec(memory_space=pltpu.VMEM)
    hbm = pl.BlockSpec(memory_space=pl.ANY)
    dma = pltpu.SemaphoreType.DMA
    tiles = n_keys // KEY_TILE
    return pl.pallas_call(
        functools.partial(attend_kernel, n_keys, heads),
        out_shape=jax.ShapeDtypeStruct((rows, 2 * heads * HEAD_DIM), BF16),
        in_specs=[vm, vm, vm, hbm, hbm],
        out_specs=vm,
        scratch_shapes=[
            pltpu.VMEM((heads, n_keys, 128), BF16), pltpu.VMEM((heads, 128, n_keys), BF16),
            pltpu.VMEM((tiles, KEY_TILE, 512), F32), pltpu.VMEM((tiles, KEY_TILE, 512), F32),
            pltpu.VMEM((2, rows, 512), F32),
            pltpu.VMEM((8, 512), F32), pltpu.VMEM((8, 512), F32), pltpu.VMEM((8, 512), F32), pltpu.VMEM((128, 512), F32),
            pltpu.VMEM((3, heads, 128, 256), BF16),
            pltpu.VMEM((2, heads, 2, 136, 256), F32), pltpu.VMEM((2, heads, 136, 256), F32),
            pltpu.VMEM((heads, 136, 256), F32), pltpu.VMEM((heads, 136, 256), F32),
            pltpu.VMEM((2, 2, PREP * heads, 128), BF16), pltpu.VMEM((2, PREP * heads, 128), F32),
            dma((2, 2)), dma((3, heads)), dma((3, heads)), dma((2, heads)), dma((2, heads)), dma((heads,)), dma((heads,)),
        ],
        compiler_params=pltpu.CompilerParams(vmem_limit_bytes=60 * 2**20, collective_id=0, has_side_effects=True),
    )(q_own, k_new, v_new, k_cache.reshape(n_keys * heads, 128), v_cache.reshape(n_keys * heads, 128))


def solution(mesh):
    cp_size = mesh.shape['cp']
    row_spec = P(('dp', 'cp'), None)
    cache_spec = P(('dp', 'cp'), None, None)
    whole = P()

    def device_step(x_rows, k_cache, v_cache, ln_gain, w_q, w_k, w_v, w_o, q_gain, k_gain):
        rows = x_rows.shape[0]
        prefix_len = k_cache.shape[0] * cp_size
        kv_heads = k_cache.shape[1]
        row_ids = lax.axis_index('cp') * rows + jnp.arange(rows)
        x_wide = x_rows.astype(F32)
        q_rot, k_new, v_new = project_rows(x_wide, ln_gain, w_q, w_k, w_v, q_gain, k_gain, prefix_len + row_ids)
        q_own = q_rot.reshape(rows, kv_heads, 2, HEAD_DIM).transpose(1, 3, 2, 0).reshape(kv_heads, HEAD_DIM, 2 * rows)
        att = attend(q_own, k_new.transpose(1, 0, 2), v_new.transpose(1, 2, 0), k_cache, v_cache)
        out = (x_wide + jnp.dot(att, w_o, preferred_element_type=F32)).astype(BF16)
        return out, k_new, v_new

    return jax.shard_map(device_step, mesh=mesh, in_specs=(row_spec, cache_spec, cache_spec, whole, whole, whole, whole, whole, whole, whole), out_specs=(row_spec, cache_spec, cache_spec), check_vma=False)
```

time: 366 us -> 102 us (0.28)
  matrix products: 158 us -> 16.4 us
  Pallas kernels: 0 us -> 75.3 us
  waiting for transfers between devices: 67.5 us -> 0 us
  other arithmetic: 69.8 us -> 5.27 us
  local copies, waits for them, and re-layouts: 34.5 us -> 3.85 us
  between operations: 14.1 us -> 0.84 us
  blocking collectives: 12.7 us -> 0 us
  starting transfers between devices: 4.98 us -> 0 us
    dot_general x20 -> x4, matrix products: 158 us -> 16.4 us  [the longest x1 5.66 us: device_step(): out = (x_wide + jnp.dot(att, w_o, preferred_element_type=F32)).astype(BF16)]
    pallas_call x0 -> x1, Pallas kernels: none -> 75.3 us  [attend(): pl.pallas_call(functools.partial(attend_kernel, n_keys, heads), out_shape...]
    reduce_sum x11 -> x0, other arithmetic: 62.6 us -> none  [the longest x8 56.7 us: partial_attend(): return (peak, jnp.sum(weights, axis=-1), weighted)]
    all_to_all x1 -> x0, waiting for transfers between devices: 43.9 us -> none  [device_step(): lax.all_to_all(piece, 'cp', 0, 0, tiled=True)]
    all_gather x3 -> x0, waiting for transfers between devices: 23.5 us -> none  [the longest x1 21.7 us: device_step(): every_q = lax.all_gather(q_grp, 'cp')]
    unnamed x19 -> x11, local copies, waits for them, and re-layouts: 17.1 us -> 1.97 us
    dynamic_slice x16 -> x0, local copies, waits for them, and re-layouts: 14.5 us -> none  [device_step(): lax.map(block_work, (every_q, every_k, every_v, jnp.arange(cp_size)))]
    all_to_all x2 -> x0, blocking collectives: 12.7 us -> none  [device_step(): lax.all_to_all(piece, 'cp', 0, 0, tiled=True)]
  transfers between devices with their start and end apart: 4 -> 0, of which waited for: 3 -> 0; matrix products, arithmetic and copies ran while one was open for 9% -> 0% of each run, Pallas kernels for 0% -> 0%
where the time goes in v1:
time: 102 us
  Pallas kernels  75.3 us (74%)
  matrix products  16.4 us (16%)
  other arithmetic  5.27 us (5%)
  local copies, waits for them, and re-layouts  3.85 us (4%)
    pallas_call x1, Pallas kernels, attend(): pl.pallas_call(functools.partial(attend_kernel, n_keys, heads), out_shape...  75.3 us
    dot_general x1, matrix products, device_step(): out = (x_wide + jnp.dot(att, w_o, preferred_element_type=F32)).astype(BF16)  5.66 us
    dot_general x1, matrix products, project_rows(): jnp.dot(hidden, w_q, preferred_element_type=F32).astype(BF16)  4.87 us
    dot_general x1, matrix products, project_rows(): jnp.dot(hidden, w_v, preferred_element_type=F32).astype(BF16)  2.95 us
    dot_general x1, matrix products, project_rows(): jnp.dot(hidden, w_k, preferred_element_type=F32).astype(BF16)  2.94 us

profile of v1, /device:TPU:0, one launch (start us, length us, event | category | flops | bytes accessed | tf_op | source)
XLA Modules:
  0.0 101.7 jit_solution(4124382787347679755)
XLA Ops:
  0.6 0.7 convert_element_type.51
  1.3 1.2 %fusion.4 = f32[128]{0:T(128)S(1)} fusion(bf16[128,2048]{1,0:T(8,128)(2,1)} %param.10), kind=kLoop, calls=%fused_computation.10 | loop fusion | flops 786304 | bytes 524800 | tf_op jit(solution)/shard_map/reduce_sum | solution.py:25
  2.6 4.9 %fusion.2 = f32[16,8,16,128]{3,1,2,0:T(8,128)S(1)} fusion(bf16[2048,2048]{1,0:T(8,128)(2,1)} %param.14, bf16[128,2048]{1,0:T(8,128)(2,1)} %param.10, f32[2048]{0:T(1024)S(1)} %convert_element_type.51, f32[128]{0:T(128)S(1)} %add_rsqrt_fusion.2), kind=kOutput, calls=%fused_computation.6 | convolution fusion | flops 1075314688 | bytes 9970176 | tf_op jit(solution)/shard_map/dot_general | solution.py:43
  7.5 0.2 copy.46
  7.7 0.4 copy.36
  8.1 0.3 multiply_reduce_fusion
  8.5 0.3 multiply_multiply_fusion
  8.8 0.2 multiply_cosine_fusion
  9.0 0.2 subtract_convert_fusion.1
  9.2 0.9 copy_bitcast_fusion.q_own
  10.0 2.9 %fusion.3 = f32[128,1024]{1,0:T(8,128)S(1)} fusion(bf16[2048,1024]{1,0:T(8,128)(2,1)} %param.15, bf16[128,2048]{1,0:T(8,128)(2,1)S(1)} %copy-done, f32[2048]{0:T(1024)S(1)} %convert_element_type.51, f32[128]{0:T(128)S(1)} %add_rsqrt_fusion.2), kind=kOutput, calls=%fused_computation.9 | convolution fusion | flops 538181632 | bytes 5251584 | tf_op jit(solution)/shard_map/dot_general | solution.py:44
  13.0 0.2 copy.38
  13.2 0.2 copy.39
  13.5 0.2 multiply_multiply_fusion.1
  13.8 0.1 copy.40
  13.9 0.3 subtract_convert_fusion
  14.1 0.9 fusion.15.k_new
  15.0 2.9 %convolution_convert_fusion.1 = bf16[128,1024]{1,0:T(8,128)(2,1)S(1)} fusion(bf16[2048,1024]{1,0:T(8,128)(2,1)} %param.16, bf16[128,2048]{1,0:T(8,128)(2,1)S(1)} %copy-done, f32[2048]{0:T(1024)S(1)} %convert_element_type.51, f32[128]{0:T(128)S(1)} %add_rsqrt_fusion.2), kind=kOutput, calls=%fused_computation.7 | convolution fusion | flops 538050560 | bytes 4989440 | tf_op jit(solution)/shard_map/dot_general | solution.py:45
  18.0 0.8 copy.42
  18.8 75.3 %shard_map.121 = bf16[128,2048]{1,0:T(8,128)(2,1)} custom-call(bf16[8,128,256]{2,1,0:T(8,128)(2,1)} %copy_bitcast_fusion.q_own, bf16[8,128,128]{2,1,0:T(8,128)(2,1)} %fusion.15.k_new, bf16[8,128,128]{2,1,0:T(8,128)(2,1)} %bitcast.30, bf16[32768,128]{1,0:T(8,128)(2,1)} %bitcast.27, bf16[32768,128]{1,0:T(8,128)(2,1)} %bitcast.28), custom_call_target="tpu_custom_call" | custom-call | tf_op jit(solution)/shard_map/pallas_call | solution.py:267
  94.1 5.7 %fusion.1 = bf16[128,2048]{1,0:T(8,128)(2,1)} fusion(bf16[128,2048]{1,0:T(8,128)(2,1)} %shard_map.121, bf16[2048,2048]{1,0:T(8,128)(2,1)} %param.17, bf16[128,2048]{1,0:T(8,128)(2,1)S(1)} %copy-done), kind=kOutput, calls=%fused_computation.3 | convolution fusion | flops 1074528256 | bytes 9961472 | tf_op jit(solution)/shard_map/dot_general | solution.py:302
  99.8 0.1 pad_maximum_fusion
  99.9 0.9 copy.43
  100.8 0.9 copy.44
  (18 shorter events, 0.3 us)
Async XLA Ops:
  2.6 5.5 %copy-start.2 = (bf16[128]{0:T(256)(128)(2,1)S(1)}, bf16[128]{0:T(256)(128)(2,1)}, u32[]{:S(2)}) copy-start(bf16[128]{0:T(256)(128)(2,1)} %param.18) | copy-start | bytes 772
  7.4 2.6 %copy-start = (bf16[128,2048]{1,0:T(8,128)(2,1)S(1)}, bf16[128,2048]{1,0:T(8,128)(2,1)}, u32[]{:S(2)}) copy-start(bf16[128,2048]{1,0:T(8,128)(2,1)} %param.10) | copy-start | bytes 1572868
  7.5 5.9 %copy-start.3 = (bf16[128]{0:T(256)(128)(2,1)S(1)}, bf16[128]{0:T(256)(128)(2,1)}, u32[]{:S(2)}) copy-start(bf16[128]{0:T(256)(128)(2,1)} %param.19) | copy-start | bytes 772
  94.1 6.7 %copy-start.1 = (bf16[128,1024]{0,1:T(8,128)(2,1)S(1)}, bf16[128,1024]{0,1:T(8,128)(2,1)}, u32[]{:S(2)}) copy-start(bf16[128,1024]{0,1:T(8,128)(2,1)} %copy.42) | copy-start | bytes 786436

commit v2 on v1

v2 whole, which is shorter than its diff:
```python
import functools
import math

import jax
import jax.numpy as jnp
from jax import lax
from jax.experimental import pallas as pl
from jax.experimental.pallas import tpu as pltpu
from jax.sharding import PartitionSpec as P

HEAD_DIM = 128
ROPE_THETA = 1.0e6
NORM_EPS = 1.0e-6
SCALE_LOG2 = HEAD_DIM ** -0.5 * math.log2(math.e)
F32, BF16 = jnp.float32, jnp.bfloat16
MESH = pl.DeviceIdType.MESH

KEY_TILE = 256
PREP = 256
GROUP = 8
LEAD = 3


def rope_tables(positions):
    half = HEAD_DIM // 2
    inv_freq = ROPE_THETA ** (-jnp.arange(half, dtype=F32) * (2.0 / HEAD_DIM))
    angles = positions.astype(F32)[:, None] * inv_freq[None, :]
    cos_tab, sin_tab = jnp.cos(angles), jnp.sin(angles)
    return jnp.concatenate([cos_tab, cos_tab], axis=1), jnp.concatenate([-sin_tab, sin_tab], axis=1)


def block_kernel(n_keys, heads, x_ref, ln_gain, q_gain, k_gain, cos_tab, sin_tab, w_q, w_k, w_v, w_o, k_hbm, v_hbm,
                 out_ref, k_out, v_out,
                 hid, wbuf, att, q_own, k_new, v_new,
                 kh, vt, sA, sB, sN, mbuf, lbuf, mcb, obuf, q_recv, part, sib_recv, comb, mir_recv, raw, wide,
                 copy_sem, w_sem, q_send, q_sem, sib_send, sib_sem, mir_send, mir_sem):
    SB = (sA, sB)
    me = lax.axis_index("cp")
    sibling = me + 1 - 2 * lax.rem(me, 2)
    mirror = lax.rem(me + 2, 4)
    rows = 128
    tiles = n_keys // KEY_TILE
    units = 2 * heads
    TS = lambda t: slice(t * 256, (t + 1) * 256)

    def remote(src, dst, send, recv, to):
        return pltpu.make_async_remote_copy(src_ref=src, dst_ref=dst, send_sem=send, recv_sem=recv,
                                            device_id={"cp": to}, device_id_type=MESH)

    def cache_copy(i, which, slot):
        src = (k_hbm, v_hbm)[which]
        n = PREP * heads
        return pltpu.make_async_copy(src.at[pl.ds(pl.multiple_of(i * n, n), n), :], raw.at[which, slot], copy_sem.at[which, slot])

    WSLOTS = 4

    def weight_copy(w, c, slot):
        return pltpu.make_async_copy(w.at[:, pl.ds(pl.multiple_of(c * 256, 256), 256)], wbuf.at[slot], w_sem.at[slot])

    for c in range(WSLOTS):
        weight_copy(w_q, c, c).start()
    for s in range(2):
        cache_copy(s, 0, s).start()
        cache_copy(s, 1, s).start()

    xw = x_ref[...].astype(F32)
    mean_sq = jnp.mean(xw * xw, axis=-1, keepdims=True)
    hid[...] = (xw * lax.rsqrt(mean_sq + NORM_EPS) * ln_gain[...]).astype(BF16)

    barrier = pltpu.get_barrier_semaphore()
    for peer in (sibling, mirror):
        pl.semaphore_signal(barrier, inc=1, device_id={"cp": peer}, device_id_type=MESH)
    pl.semaphore_wait(barrier, 2)

    def q_to_sibling(g):
        return remote(q_own.at[g], q_recv.at[0, g], q_send.at[0, g], q_sem.at[0, g], sibling)
    def q_to_mirror(g):
        return remote(q_own.at[g], q_recv.at[1, g], q_send.at[1, g], q_sem.at[1, g], mirror)
    def q_forward(g):
        return remote(q_recv.at[1, g], q_recv.at[2, g], q_send.at[2, g], q_sem.at[2, g], sibling)
    def prep(i):
        slot = lax.rem(i, 2)
        row = pl.ds(pl.multiple_of(i * PREP, PREP), PREP)
        wide[0] = raw[0, slot].astype(F32)
        for h in range(heads):
            kh[h, row, :] = wide[0, pl.ds(h, PREP, stride=heads), :].astype(BF16)
        wide[1] = raw[1, slot].astype(F32)
        for h in range(heads):
            vt[h, :, row] = wide[1, pl.ds(h, PREP, stride=heads), :].T.astype(BF16)

    def head_rows(vals, gain):
        vals = vals.astype(BF16).astype(F32)
        normed = vals * lax.rsqrt(jnp.mean(vals * vals, axis=-1, keepdims=True) + NORM_EPS) * gain
        return normed * cos_tab[...] + pltpu.roll(normed, HEAD_DIM // 2, 1) * sin_tab[...]

    def load_step(i):
        wslot = lax.rem(i, WSLOTS)
        slot = lax.rem(i, 2)
        pltpu.make_async_copy(w_q.at[:, pl.ds(0, 256)], wbuf.at[wslot], w_sem.at[wslot]).wait()
        cache_copy(i, 0, slot).wait()
        cache_copy(i, 1, slot).wait()
        raw_cols = jnp.dot(hid[...], wbuf[wslot], preferred_element_type=F32)
        prep(i)
        return raw_cols

    def next_loads(i, w, c):
        if w is not None:
            weight_copy(w, c, lax.rem(i, WSLOTS)).start()
        @pl.when(i + 2 < n_keys // PREP)
        def _():
            cache_copy(i + 2, 0, lax.rem(i, 2)).start()
            cache_copy(i + 2, 1, lax.rem(i, 2)).start()

    n_q, n_kv = heads, heads // 2

    def q_step(i, w, c):
        cols = load_step(i)
        for j in range(2):
            r = head_rows(cols[:, j * 128:(j + 1) * 128], q_gain[...])
            q_own[i, :, j * 128:(j + 1) * 128] = r.T.astype(BF16)
        q_to_mirror(i).start()
        q_to_sibling(i).start()
        next_loads(i, w, c)

    def q_steps(lo, hi, w, off):
        def run(i, _):
            q_step(i, w, i - off)
            return 0
        lax.fori_loop(lo, hi, run, 0)
    q_steps(0, n_q - WSLOTS, w_q, -WSLOTS)
    q_steps(n_q - WSLOTS, n_q, w_k, n_q - WSLOTS)

    def k_step(c, _):
        cols = load_step(n_q + c)
        for j in range(2):
            r = head_rows(cols[:, j * 128:(j + 1) * 128], k_gain[...])
            k_new[2 * c + j] = r.astype(BF16)
        next_loads(n_q + c, w_v, c)
        return 0
    lax.fori_loop(0, n_kv, k_step, 0)

    def v_step(c, _):
        cols = load_step(n_q + n_kv + c)
        for j in range(2):
            v_new[2 * c + j] = cols[:, j * 128:(j + 1) * 128].T.astype(BF16)
        next_loads(n_q + n_kv + c, None, 0)
        return 0
    lax.fori_loop(0, n_kv, v_step, 0)
    for c in range(WSLOTS):
        weight_copy(w_o, c, c).start()

    for h in range(heads):
        wide[0, pl.ds(h, rows, stride=heads), :] = k_new[h].astype(F32)
        wide[1, pl.ds(h, rows, stride=heads), :] = v_new[h].astype(F32).T
    k_out[...] = wide[0, 0:rows * heads, :].astype(BF16)
    v_out[...] = wide[1, 0:rows * heads, :].astype(BF16)

    q_to_mirror(0).wait_recv()
    q_forward(0).start()
    q_to_sibling(0).wait_recv()
    q_forward(0).wait_recv()

    def sib_copy(kind, g):
        return remote(part.at[kind, g, 1], sib_recv.at[kind, g], sib_send.at[kind, g], sib_sem.at[kind, g], sibling)
    def mir_copy(g):
        return remote(comb.at[g], mir_recv.at[g], mir_send.at[g], mir_sem.at[g], mirror)

    def main_body():
        def q_cols(kind, g):
            if kind == 0:
                return jnp.concatenate([q_recv[1, g], q_recv[2, g]], axis=1)
            return jnp.concatenate([q_own[g], q_recv[0, g]], axis=1)

        def dot(a, b):
            return lax.dot_general(a, b, (((1,), (0,)), ((), ())), preferred_element_type=F32)

        def col_max(mx, s):
            return jnp.maximum(mx, jnp.max(s.reshape(s.shape[0] // 8, 8, 512), axis=0))

        def qk(q, g, kc, slot, mx):
            s = dot(kh[g, pl.ds(pl.multiple_of(kc * KEY_TILE, KEY_TILE), KEY_TILE), :], q)
            SB[slot][kc] = s
            return col_max(mx, s)

        def qk_new(q, kind, g, slot, mx):
            own, other = (me, sibling) if kind == 1 else (mirror, lax.rem(sibling + 2, 4))
            key = lax.broadcasted_iota(jnp.int32, (rows, 512), 0) + me * rows
            col = lax.broadcasted_iota(jnp.int32, (rows, 512), 1)
            row = lax.rem(col, rows) + jnp.where(col < 256, own, other) * rows
            s = jnp.where(key <= row, dot(k_new[g], q), -jnp.inf)
            sN[slot] = s
            return col_max(mx, s)

        def weights(s, mc, ls):
            p = jnp.exp2(s * SCALE_LOG2 - mc)
            return p.astype(BF16), ls + jnp.sum(p.reshape(s.shape[0] // 8, 8, 512), axis=0)

        def block(last, kind_n, g_n, g, b, par):
            steps = [("Q", i) for i in range(GROUP)] + [("Q", None)] * last
            for i in range(GROUP):
                steps.insert(LEAD + 2 * i, ("P", i))
            steps += [("P", None)] * last
            mx, ls, mc = mbuf[...], lbuf[...], mcb[par, 0:1, :]
            q = q_cols(kind_n, g_n)
            acc = None
            for op, i in steps:
                if op == "Q" and i is None:
                    mx = qk_new(q, kind_n, g_n, 1 - par, mx)
                elif op == "Q":
                    mx = qk(q, g_n, b * GROUP + i, 1 - par, mx)
                else:
                    if i is None:
                        p, ls = weights(sN[par], mc, ls)
                        v = v_new[g]
                    else:
                        kc = b * GROUP + i
                        p, ls = weights(SB[par][kc], mc, ls)
                        v = vt[g, :, pl.ds(pl.multiple_of(kc * KEY_TILE, KEY_TILE), KEY_TILE)]
                    pv = dot(v, p)
                    acc = pv if acc is None else acc + pv
            if not last:
                mbuf[...] = mx
                lbuf[...] = ls
                obuf[...] = acc
                return
            acc = obuf[...] + acc
            total = jnp.sum(ls, axis=0, keepdims=True)
            for t in range(2):
                part[par, g, t, 0:128, :] = acc[:, TS(t)]
                part[par, g, t, 128:129, :] = mc[:, TS(t)]
                part[par, g, t, 129:130, :] = total[:, TS(t)]
            mcb[1 - par, 0:1, :] = jnp.max(mx, axis=0, keepdims=True) * SCALE_LOG2
            mbuf[...] = jnp.full(mbuf.shape, -jnp.inf, F32)
            lbuf[...] = jnp.zeros(lbuf.shape, F32)

        def merge(a, b):
            ma, mb = a[128:129, :], b[128:129, :]
            m = jnp.maximum(ma, mb)
            fa, fb = jnp.exp2(ma - m), jnp.exp2(mb - m)
            return a[0:128, :] * fa + b[0:128, :] * fb, m, a[129:130, :] * fa + b[129:130, :] * fb

        def unit(g, kind):
            kind_n, g_n = (1, g) if kind == 0 else (0, jnp.minimum(g + 1, heads - 1))
            @pl.when(g < 2 * heads)
            def _():
                block(False, kind_n, g_n, g, 0, kind)
            if kind == 1:
                sib_copy(0, g).wait_recv()
                acc, m, total = merge(part.at[0, g, 0], sib_recv.at[0, g])
                comb[g, 0:128, :] = acc
                comb[g, 128:129, :] = m
                comb[g, 129:130, :] = total
                mir_copy(g).start()
            @pl.when(g < 3 * heads)
            def _():
                block(True, kind_n, g_n, g, 1, kind)
            sib_copy(kind, g).start()

        mbuf[...] = jnp.full(mbuf.shape, -jnp.inf, F32)
        q0 = q_cols(0, 0)
        def first(b, _):
            mx = mbuf[...]
            for c in range(4):
                mx = qk(q0, 0, 4 * b + c, 0, mx)
            mbuf[...] = mx
            return 0
        lax.fori_loop(0, tiles // 4, first, 0)
        mx = qk_new(q0, 0, 0, 0, mbuf[...])
        mcb[0, 0:1, :] = jnp.max(mx, axis=0, keepdims=True) * SCALE_LOG2
        mbuf[...] = jnp.full(mbuf.shape, -jnp.inf, F32)
        lbuf[...] = jnp.zeros(lbuf.shape, F32)

        def body(g, _):
            @pl.when(g + 1 < heads)
            def _():
                q_to_mirror(g + 1).wait_recv()
                q_forward(g + 1).start()
            unit(g, 0)
            @pl.when(g + 1 < heads)
            def _():
                q_to_sibling(g + 1).wait_recv()
                q_forward(g + 1).wait_recv()
            unit(g, 1)
            return 0
        lax.fori_loop(0, heads, body, 0)

        def final(g, _):
            sib_copy(1, g).wait_recv()
            mir_copy(g).wait_recv()
            acc, m, total = merge(part.at[1, g, 0], sib_recv.at[1, g])
            mb = mir_recv[g, 128:129, :]
            top = jnp.maximum(m, mb)
            fa, fb = jnp.exp2(m - top), jnp.exp2(mb - top)
            acc = acc * fa + mir_recv[g, 0:128, :] * fb
            total = total * fa + mir_recv[g, 129:130, :] * fb
            o = acc / total
            for j in range(2):
                cols = pl.ds(pl.multiple_of((2 * g + j) * 128, 128), 128)
                att[:, cols] = o[:, j * 128:(j + 1) * 128].T.astype(BF16)
            return 0
        lax.fori_loop(0, heads, final, 0)
        n_out = x_ref.shape[1] // 256
        def project(n, _):
            slot = lax.rem(n, WSLOTS)
            weight_copy(w_o, n, slot).wait()
            cols = pl.ds(pl.multiple_of(n * 256, 256), 256)
            add = jnp.dot(att[...], wbuf[slot], preferred_element_type=F32)
            out_ref[:, cols] = (x_ref[:, cols].astype(F32) + add).astype(BF16)
            @pl.when(n + WSLOTS < n_out)
            def _():
                weight_copy(w_o, n + WSLOTS, slot).start()
            return 0
        lax.fori_loop(0, n_out, project, 0)

    main_body()

    def drain(g, _):
        q_to_mirror(g).wait_send()
        q_to_sibling(g).wait_send()
        q_forward(g).wait_send()
        sib_copy(0, g).wait_send()
        sib_copy(1, g).wait_send()
        mir_copy(g).wait_send()
        return 0
    lax.fori_loop(0, heads, drain, 0)


def attention_block(x, ln_gain, q_gain, k_gain, cos_tab, sin_tab, w_q, w_k, w_v, w_o, k_cache, v_cache):
    n_keys, heads, _ = k_cache.shape
    rows, width = x.shape
    vm = pl.BlockSpec(memory_space=pltpu.VMEM)
    hbm = pl.BlockSpec(memory_space=pl.ANY)
    dma = pltpu.SemaphoreType.DMA
    tiles = n_keys // KEY_TILE
    return pl.pallas_call(
        functools.partial(block_kernel, n_keys, heads),
        out_shape=(jax.ShapeDtypeStruct((rows, width), BF16), jax.ShapeDtypeStruct((rows * heads, HEAD_DIM), BF16),
                   jax.ShapeDtypeStruct((rows * heads, HEAD_DIM), BF16)),
        in_specs=[vm] * 6 + [hbm] * 6,
        out_specs=(vm, vm, vm),
        scratch_shapes=[
            pltpu.VMEM((rows, width), BF16), pltpu.VMEM((4, width, 256), BF16),
            pltpu.VMEM((rows, w_o.shape[0]), BF16), pltpu.VMEM((heads, 128, 256), BF16),
            pltpu.VMEM((heads, rows, 128), BF16), pltpu.VMEM((heads, 128, rows), BF16),
            pltpu.VMEM((heads, n_keys, 128), BF16), pltpu.VMEM((heads, 128, n_keys), BF16),
            pltpu.VMEM((tiles, KEY_TILE, 512), F32), pltpu.VMEM((tiles, KEY_TILE, 512), F32),
            pltpu.VMEM((2, rows, 512), F32),
            pltpu.VMEM((8, 512), F32), pltpu.VMEM((8, 512), F32), pltpu.VMEM((2, 8, 512), F32), pltpu.VMEM((128, 512), F32),
            pltpu.VMEM((3, heads, 128, 256), BF16),
            pltpu.VMEM((2, heads, 2, 136, 256), F32), pltpu.VMEM((2, heads, 136, 256), F32),
            pltpu.VMEM((heads, 136, 256), F32), pltpu.VMEM((heads, 136, 256), F32),
            pltpu.VMEM((2, 2, PREP * heads, 128), BF16), pltpu.VMEM((2, PREP * heads, 128), F32),
            dma((2, 2)), dma((4,)), dma((3, heads)), dma((3, heads)), dma((2, heads)), dma((2, heads)), dma((heads,)), dma((heads,)),
        ],
        compiler_params=pltpu.CompilerParams(vmem_limit_bytes=67043328, collective_id=0, has_side_effects=True),
    )(x, ln_gain, q_gain, k_gain, cos_tab, sin_tab, w_q, w_k, w_v, w_o,
      k_cache.reshape(n_keys * heads, HEAD_DIM), v_cache.reshape(n_keys * heads, HEAD_DIM))


def solution(mesh):
    cp_size = mesh.shape['cp']
    row_spec = P(('dp', 'cp'), None)
    cache_spec = P(('dp', 'cp'), None, None)
    whole = P()

    def device_step(x_rows, k_cache, v_cache, ln_gain, w_q, w_k, w_v, w_o, q_gain, k_gain):
        rows = x_rows.shape[0]
        n_keys, heads, _ = k_cache.shape
        positions = n_keys * cp_size + lax.axis_index('cp') * rows + jnp.arange(rows)
        cos_tab, sin_tab = rope_tables(positions)
        wide_row = lambda v: v.astype(F32)[None, :]
        out, k_new, v_new = attention_block(x_rows, wide_row(ln_gain), wide_row(q_gain), wide_row(k_gain), cos_tab, sin_tab,
                                            w_q, w_k, w_v, w_o, k_cache, v_cache)
        return out, k_new.reshape(rows, heads, HEAD_DIM), v_new.reshape(rows, heads, HEAD_DIM)

    return jax.shard_map(device_step, mesh=mesh, in_specs=(row_spec, cache_spec, cache_spec, whole, whole, whole, whole, whole, whole, whole), out_specs=(row_spec, cache_spec, cache_spec), check_vma=False)
```

time: 102 us -> 83.2 us (0.82)
  matrix products: 16.4 us -> 0 us
  Pallas kernels: 75.3 us -> 73.2 us
  other arithmetic: 5.27 us -> 3.62 us
  local copies, waits for them, and re-layouts: 3.85 us -> 5.22 us
    dot_general x4 -> x0, matrix products: 16.4 us -> none  [the longest x1 5.66 us: device_step(): out = (x_wide + jnp.dot(att, w_o, preferred_element_type=F32)).astype(BF16)]
    unnamed x11 -> x3, local copies, waits for them, and re-layouts: 1.97 us -> 5.22 us
    broadcast_in_dim x0 -> x2, other arithmetic: none -> 2.55 us  [device_step(): wide_row = lambda v: v.astype(F32)[None, :]]
    pallas_call x1, Pallas kernels: 75.3 us -> 73.2 us  [attention_block(): pl.pallas_call(functools.partial(block_kernel, n_keys, heads), out_shape=...]
    convert_element_type x4 -> x0, local copies, waits for them, and re-layouts: 1.65 us -> none  [the longest x1 0.84 us: project_rows(): jnp.dot(hidden, w_v, preferred_element_type=F32).astype(BF16)]
    reduce_sum x3 -> x0, other arithmetic: 1.61 us -> none  [rms_norm(): mean_sq = jnp.mean(vals * vals, axis=-1, keepdims=True)]
where the time goes in v2:
time: 83.2 us; the launch traced here: 82.7 us
  Pallas kernels  73.2 us (88%)
  local copies, waits for them, and re-layouts  5.22 us (6%)
  other arithmetic  3.62 us (4%)
    pallas_call x1, Pallas kernels, attention_block(): pl.pallas_call(functools.partial(block_kernel, n_keys, heads), out_shape=...  73.2 us
    unnamed x3, local copies, waits for them, and re-layouts  5.22 us
    broadcast_in_dim x2, other arithmetic, device_step(): wide_row = lambda v: v.astype(F32)[None, :]  2.55 us

profile of v2, /device:TPU:0, one launch (start us, length us, event | category | flops | bytes accessed | tf_op | source)
XLA Modules:
  0.0 82.7 jit_solution(14172229225409522385)
XLA Ops:
  0.7 1.3 %bitcast_convert_fusion = (f32[1,128]{1,0:T(1,128)}, f32[1,128]{1,0:T(1,128)}) fusion(bf16[128]{0:T(256)(128)(2,1)} %param.19, bf16[128]{0:T(256)(128)(2,1)} %param.18), kind=kLoop, calls=%fused_computation.5 | loop fusion | flops 256 | bytes 1536 | tf_op jit(solution)/shard_map/broadcast_in_dim | solution.py:371
  1.9 1.3 %broadcast_in_dim.23 = f32[2048]{0:T(1024)} convert(bf16[2048]{0:T(1024)(128)(2,1)} %param.13) | non-fusion elementwise | flops 2048 | bytes 12288 | tf_op jit(solution)/shard_map/broadcast_in_dim | solution.py:371
  3.2 0.3 fusion
  3.5 0.8 pad_maximum_fusion
  4.3 73.2 %shard_map.121 = (bf16[128,2048]{1,0:T(8,128)(2,1)}, bf16[1024,128]{1,0:T(8,128)(2,1)}, bf16[1024,128]{1,0:T(8,128)(2,1)}) custom-call(bf16[128,2048]{1,0:T(8,128)(2,1)} %x_ref.1, f32[1,2048]{1,0:T(1,128)} %bitcast.15, f32[1,128]{1,0:T(1,128)} %get-tuple-element.15.q_gain, f32[1,128]{1,0:T(1,128)} %get-tuple-element.14.k_gain, ...), custom_call_target="tpu_custom_call" | custom-call | tf_op jit(solution)/shard_map/pallas_call | solution.py:335
  77.4 1.9 %copy.16 = bf16[128,2048]{1,0:T(8,128)(2,1)} copy(bf16[128,2048]{1,0:T(8,128)(2,1)} %get-tuple-element.19) | data formatting | bytes 1048576
  79.3 1.7 %copy.17 = bf16[128,8,128]{2,1,0:T(8,128)(2,1)} copy(bf16[128,8,128]{2,1,0:T(8,128)(2,1)} %bitcast.14) | data formatting | bytes 524288
  81.0 1.7 %copy.18 = bf16[128,8,128]{2,1,0:T(8,128)(2,1)} copy(bf16[128,8,128]{2,1,0:T(8,128)(2,1)} %bitcast.13) | data formatting | bytes 524288
  (2 shorter events, 0.0 us)

commit v3 on v2

--- a/solution.py
+++ b/solution.py
@@ -17,22 +17,21 @@
 
 KEY_TILE = 256
 PREP = 256
-GROUP = 8
-LEAD = 3
+GROUP = 16
+LEAD = 1
 
 
 def rope_tables(positions):
     half = HEAD_DIM // 2
     inv_freq = ROPE_THETA ** (-jnp.arange(half, dtype=F32) * (2.0 / HEAD_DIM))
     angles = positions.astype(F32)[:, None] * inv_freq[None, :]
-    cos_tab, sin_tab = jnp.cos(angles), jnp.sin(angles)
-    return jnp.concatenate([cos_tab, cos_tab], axis=1), jnp.concatenate([-sin_tab, sin_tab], axis=1)
+    return jnp.cos(angles), jnp.sin(angles)
 
 
 def block_kernel(n_keys, heads, x_ref, ln_gain, q_gain, k_gain, cos_tab, sin_tab, w_q, w_k, w_v, w_o, k_hbm, v_hbm,
                  out_ref, k_out, v_out,
-                 hid, wbuf, att, q_own, k_new, v_new,
-                 kh, vt, sA, sB, sN, mbuf, lbuf, mcb, obuf, q_recv, part, sib_recv, comb, mir_recv, raw, wide,
+                 hid, wbuf, cols, cosw, sinw, att, k_new, v_new,
+                 kh, vt, sA, sB, sN, mbuf, lbuf, mcb, obuf, qs, part, sib_recv, comb, mir_recv, raw, wide,
                  copy_sem, w_sem, q_send, q_sem, sib_send, sib_sem, mir_send, mir_sem):
     SB = (sA, sB)
     me = lax.axis_index("cp")
@@ -65,7 +64,9 @@
 
     xw = x_ref[...].astype(F32)
     mean_sq = jnp.mean(xw * xw, axis=-1, keepdims=True)
-    hid[...] = (xw * lax.rsqrt(mean_sq + NORM_EPS) * ln_gain[...]).astype(BF16)
+    hid[...] = (xw * lax.rsqrt(mean_sq + NORM_EPS) * ln_gain[...].astype(F32).reshape(1, -1)).astype(BF16)
+    cosw[...] = jnp.concatenate([cos_tab[...], cos_tab[...]], axis=1)
+    sinw[...] = jnp.concatenate([-sin_tab[...], sin_tab[...]], axis=1)
 
     barrier = pltpu.get_barrier_semaphore()
     for peer in (sibling, mirror):
@@ -73,11 +74,12 @@
     pl.semaphore_wait(barrier, 2)
 
     def q_to_sibling(g):
-        return remote(q_own.at[g], q_recv.at[0, g], q_send.at[0, g], q_sem.at[0, g], sibling)
+        return remote(qs.at[0, g], qs.at[1, g], q_send.at[0, g], q_sem.at[0, g], sibling)
     def q_to_mirror(g):
-        return remote(q_own.at[g], q_recv.at[1, g], q_send.at[1, g], q_sem.at[1, g], mirror)
+        return remote(qs.at[0, g], qs.at[2, g], q_send.at[1, g], q_sem.at[1, g], mirror)
     def q_forward(g):
-        return remote(q_recv.at[1, g], q_recv.at[2, g], q_send.at[2, g], q_sem.at[2, g], sibling)
+        return remote(qs.at[2, g], qs.at[3, g], q_send.at[2, g], q_sem.at[2, g], sibling)
+
     def prep(i):
         slot = lax.rem(i, 2)
         row = pl.ds(pl.multiple_of(i * PREP, PREP), PREP)
@@ -91,63 +93,66 @@
     def head_rows(vals, gain):
         vals = vals.astype(BF16).astype(F32)
         normed = vals * lax.rsqrt(jnp.mean(vals * vals, axis=-1, keepdims=True) + NORM_EPS) * gain
-        return normed * cos_tab[...] + pltpu.roll(normed, HEAD_DIM // 2, 1) * sin_tab[...]
-
-    def load_step(i):
+        return normed * cosw[...] + pltpu.roll(normed, HEAD_DIM // 2, 1) * sinw[...]
+
+    n_q, n_kv = heads, heads // 2
+    steps = n_q + 2 * n_kv
+
+    def load_step(i, post):
         wslot = lax.rem(i, WSLOTS)
         slot = lax.rem(i, 2)
-        pltpu.make_async_copy(w_q.at[:, pl.ds(0, 256)], wbuf.at[wslot], w_sem.at[wslot]).wait()
+        weight_copy(w_q, 0, wslot).wait()
         cache_copy(i, 0, slot).wait()
         cache_copy(i, 1, slot).wait()
-        raw_cols = jnp.dot(hid[...], wbuf[wslot], preferred_element_type=F32)
+        done = cols[...]
+        fresh = jnp.dot(hid[...], wbuf[wslot], preferred_element_type=F32)
         prep(i)
-        return raw_cols
-
-    def next_loads(i, w, c):
-        if w is not None:
-            weight_copy(w, c, lax.rem(i, WSLOTS)).start()
+        post(i - 1, done)
+        cols[...] = fresh
+        ahead = i + WSLOTS
+        for w, lo, hi in ((w_q, 0, n_q), (w_k, n_q, n_q + n_kv), (w_v, n_q + n_kv, steps), (w_o, steps, steps + WSLOTS)):
+            @pl.when((ahead >= lo) & (ahead < hi))
+            def _():
+                weight_copy(w, ahead - lo, wslot).start()
         @pl.when(i + 2 < n_keys // PREP)
         def _():
-            cache_copy(i + 2, 0, lax.rem(i, 2)).start()
-            cache_copy(i + 2, 1, lax.rem(i, 2)).start()
-
-    n_q, n_kv = heads, heads // 2
-
-    def q_step(i, w, c):
-        cols = load_step(i)
-        for j in range(2):
-            r = head_rows(cols[:, j * 128:(j + 1) * 128], q_gain[...])
-            q_own[i, :, j * 128:(j + 1) * 128] = r.T.astype(BF16)
-        q_to_mirror(i).start()
-        q_to_sibling(i).start()
-        next_loads(i, w, c)
-
-    def q_steps(lo, hi, w, off):
-        def run(i, _):
-            q_step(i, w, i - off)
-            return 0
-        lax.fori_loop(lo, hi, run, 0)
-    q_steps(0, n_q - WSLOTS, w_q, -WSLOTS)
-    q_steps(n_q - WSLOTS, n_q, w_k, n_q - WSLOTS)
-
-    def k_step(c, _):
-        cols = load_step(n_q + c)
-        for j in range(2):
-            r = head_rows(cols[:, j * 128:(j + 1) * 128], k_gain[...])
-            k_new[2 * c + j] = r.astype(BF16)
-        next_loads(n_q + c, w_v, c)
+            cache_copy(i + 2, 0, slot).start()
+            cache_copy(i + 2, 1, slot).start()
+
+    def halves(vals):
+        return [vals[:, j * 128:(j + 1) * 128] for j in range(2)]
+
+    def q_post(g, vals):
+        for j, half in enumerate(halves(vals)):
+            qs[0, g, :, j * 128:(j + 1) * 128] = head_rows(half, q_gain[...].astype(F32).reshape(1, -1)).T.astype(BF16)
+
+    def k_post(c, vals):
+        for j, half in enumerate(halves(vals)):
+            k_new[2 * (c - n_q) + j] = head_rows(half, k_gain[...].astype(F32).reshape(1, -1)).astype(BF16)
+
+    def v_post(c, vals):
+        for j, half in enumerate(halves(vals)):
+            v_new[2 * (c - n_q - n_kv) + j] = half.T.astype(BF16)
+
+    load_step(0, lambda i, vals: None)
+
+    def q_steps(i, _):
+        load_step(i, q_post)
+        q_to_mirror(i - 1).start()
+        q_to_sibling(i - 1).start()
         return 0
-    lax.fori_loop(0, n_kv, k_step, 0)
-
-    def v_step(c, _):
-        cols = load_step(n_q + n_kv + c)
-        for j in range(2):
-            v_new[2 * c + j] = cols[:, j * 128:(j + 1) * 128].T.astype(BF16)
-        next_loads(n_q + n_kv + c, None, 0)
+    lax.fori_loop(1, n_q + 1, q_steps, 0)
+
+    def k_steps(i, _):
+        load_step(i, k_post)
         return 0
-    lax.fori_loop(0, n_kv, v_step, 0)
-    for c in range(WSLOTS):
-        weight_copy(w_o, c, c).start()
+    lax.fori_loop(n_q + 1, n_q + n_kv + 1, k_steps, 0)
+
+    def v_steps(i, _):
+        load_step(i, v_post)
+        return 0
+    lax.fori_loop(n_q + n_kv + 1, steps, v_steps, 0)
+    v_post(steps - 1, cols[...])
 
     for h in range(heads):
         wide[0, pl.ds(h, rows, stride=heads), :] = k_new[h].astype(F32)
@@ -155,8 +160,9 @@
     k_out[...] = wide[0, 0:rows * heads, :].astype(BF16)
     v_out[...] = wide[1, 0:rows * heads, :].astype(BF16)
 
-    q_to_mirror(0).wait_recv()
-    q_forward(0).start()
+    for g in range(2):
+        q_to_mirror(g).wait_recv()
+        q_forward(g).start()
     q_to_sibling(0).wait_recv()
     q_forward(0).wait_recv()
 
@@ -167,9 +173,8 @@
 
     def main_body():
         def q_cols(kind, g):
-            if kind == 0:
-                return jnp.concatenate([q_recv[1, g], q_recv[2, g]], axis=1)
-            return jnp.concatenate([q_own[g], q_recv[0, g]], axis=1)
+            base = 2 - 2 * kind
+            return jnp.concatenate([qs[base, g], qs[base + 1, g]], axis=1)
 
         def dot(a, b):
             return lax.dot_general(a, b, (((1,), (0,)), ((), ())), preferred_element_type=F32)
@@ -183,7 +188,8 @@
             return col_max(mx, s)
 
         def qk_new(q, kind, g, slot, mx):
-            own, other = (me, sibling) if kind == 1 else (mirror, lax.rem(sibling + 2, 4))
+            own = lax.rem(me + 2 * (1 - kind), 4)
+            other = lax.rem(sibling + 2 * (1 - kind), 4)
             key = lax.broadcasted_iota(jnp.int32, (rows, 512), 0) + me * rows
             col = lax.broadcasted_iota(jnp.int32, (rows, 512), 1)
             row = lax.rem(col, rows) + jnp.where(col < 256, own, other) * rows
@@ -195,7 +201,7 @@
             p = jnp.exp2(s * SCALE_LOG2 - mc)
             return p.astype(BF16), ls + jnp.sum(p.reshape(s.shape[0] // 8, 8, 512), axis=0)
 
-        def block(last, kind_n, g_n, g, b, par):
+        def block(last, kind_n, g_n, kind, g, b, par):
             steps = [("Q", i) for i in range(GROUP)] + [("Q", None)] * last
             for i in range(GROUP):
                 steps.insert(LEAD + 2 * i, ("P", i))
@@ -226,9 +232,9 @@
             acc = obuf[...] + acc
             total = jnp.sum(ls, axis=0, keepdims=True)
             for t in range(2):
-                part[par, g, t, 0:128, :] = acc[:, TS(t)]
-                part[par, g, t, 128:129, :] = mc[:, TS(t)]
-                part[par, g, t, 129:130, :] = total[:, TS(t)]
+                part[kind, g, t, 0:128, :] = acc[:, TS(t)]
+                part[kind, g, t, 128:129, :] = mc[:, TS(t)]
+                part[kind, g, t, 129:130, :] = total[:, TS(t)]
             mcb[1 - par, 0:1, :] = jnp.max(mx, axis=0, keepdims=True) * SCALE_LOG2
             mbuf[...] = jnp.full(mbuf.shape, -jnp.inf, F32)
             lbuf[...] = jnp.zeros(lbuf.shape, F32)
@@ -239,21 +245,32 @@
             fa, fb = jnp.exp2(ma - m), jnp.exp2(mb - m)
             return a[0:128, :] * fa + b[0:128, :] * fb, m, a[129:130, :] * fa + b[129:130, :] * fb
 
-        def unit(g, kind):
-            kind_n, g_n = (1, g) if kind == 0 else (0, jnp.minimum(g + 1, heads - 1))
-            @pl.when(g < 2 * heads)
-            def _():
-                block(False, kind_n, g_n, g, 0, kind)
-            if kind == 1:
-                sib_copy(0, g).wait_recv()
-                acc, m, total = merge(part.at[0, g, 0], sib_recv.at[0, g])
-                comb[g, 0:128, :] = acc
-                comb[g, 128:129, :] = m
-                comb[g, 129:130, :] = total
-                mir_copy(g).start()
-            @pl.when(g < 3 * heads)
-            def _():
-                block(True, kind_n, g_n, g, 1, kind)
+        def send_merged(g):
+            sib_copy(0, g).wait_recv()
+            acc, m, total = merge(part.at[0, g, 0], sib_recv.at[0, g])
+            comb[g, 0:128, :] = acc
+            comb[g, 128:129, :] = m
+            comb[g, 129:130, :] = total
+            mir_copy(g).start()
+
+        def unit_of(pos):
+            half = pos // 2
+            odd = pos - 2 * half
+            local = jnp.where((odd == 0) & (half > 0) | (pos >= 2 * heads - 1), 1, 0)
+            return local, jnp.where(pos >= 2 * heads - 1, heads - 1, jnp.maximum(half - 1 + 2 * odd, 0))
+
+        def unit(p, par):
+            pos = 2 * p + par
+            kind, g = unit_of(pos)
+            kind_n, g_n = unit_of(jnp.minimum(pos + 1, 2 * heads - 1))
+            for b in range(tiles // GROUP):
+                @pl.when(p < (2 + b) * heads)
+                def _():
+                    block(b == tiles // GROUP - 1, kind_n, g_n, kind, g, b, par)
+                if b == 0:
+                    @pl.when((p == 0) if par else (p > 0))
+                    def _():
+                        send_merged(p)
             sib_copy(kind, g).start()
 
         mbuf[...] = jnp.full(mbuf.shape, -jnp.inf, F32)
@@ -270,17 +287,17 @@
         mbuf[...] = jnp.full(mbuf.shape, -jnp.inf, F32)
         lbuf[...] = jnp.zeros(lbuf.shape, F32)
 
-        def body(g, _):
-            @pl.when(g + 1 < heads)
+        def body(p, _):
+            @pl.when(p + 1 < heads)
             def _():
-                q_to_mirror(g + 1).wait_recv()
-                q_forward(g + 1).start()
-            unit(g, 0)
-            @pl.when(g + 1 < heads)
+                q_to_sibling(p + 1).wait_recv()
+                q_forward(p + 1).wait_recv()
+            unit(p, 0)
+            @pl.when(p + 2 < heads)
             def _():
-                q_to_sibling(g + 1).wait_recv()
-                q_forward(g + 1).wait_recv()
-            unit(g, 1)
+                q_to_mirror(p + 2).wait_recv()
+                q_forward(p + 2).start()
+            unit(p, 1)
             return 0
         lax.fori_loop(0, heads, body, 0)
 
@@ -340,21 +357,31 @@
         out_specs=(vm, vm, vm),
         scratch_shapes=[
             pltpu.VMEM((rows, width), BF16), pltpu.VMEM((4, width, 256), BF16),
-            pltpu.VMEM((rows, w_o.shape[0]), BF16), pltpu.VMEM((heads, 128, 256), BF16),
+            pltpu.VMEM((rows, 256), F32), pltpu.VMEM((rows, 128), F32), pltpu.VMEM((rows, 128), F32), pltpu.VMEM((rows, w_o.shape[0]), BF16),
             pltpu.VMEM((heads, rows, 128), BF16), pltpu.VMEM((heads, 128, rows), BF16),
             pltpu.VMEM((heads, n_keys, 128), BF16), pltpu.VMEM((heads, 128, n_keys), BF16),
             pltpu.VMEM((tiles, KEY_TILE, 512), F32), pltpu.VMEM((tiles, KEY_TILE, 512), F32),
             pltpu.VMEM((2, rows, 512), F32),
             pltpu.VMEM((8, 512), F32), pltpu.VMEM((8, 512), F32), pltpu.VMEM((2, 8, 512), F32), pltpu.VMEM((128, 512), F32),
-            pltpu.VMEM((3, heads, 128, 256), BF16),
+            pltpu.VMEM((4, heads, 128, 256), BF16),
             pltpu.VMEM((2, heads, 2, 136, 256), F32), pltpu.VMEM((2, heads, 136, 256), F32),
             pltpu.VMEM((heads, 136, 256), F32), pltpu.VMEM((heads, 136, 256), F32),
             pltpu.VMEM((2, 2, PREP * heads, 128), BF16), pltpu.VMEM((2, PREP * heads, 128), F32),
             dma((2, 2)), dma((4,)), dma((3, heads)), dma((3, heads)), dma((2, heads)), dma((2, heads)), dma((heads,)), dma((heads,)),
         ],
-        compiler_params=pltpu.CompilerParams(vmem_limit_bytes=67043328, collective_id=0, has_side_effects=True),
+        compiler_params=pltpu.CompilerParams(vmem_limit_bytes=62 * 2**20, collective_id=0, has_side_effects=True),
     )(x, ln_gain, q_gain, k_gain, cos_tab, sin_tab, w_q, w_k, w_v, w_o,
       k_cache.reshape(n_keys * heads, HEAD_DIM), v_cache.reshape(n_keys * heads, HEAD_DIM))
+
+
+def pass_on(*arrays):
+    def kernel(*refs):
+        n = len(refs) // 2
+        for src, dst in zip(refs[:n], refs[n:]):
+            dst[...] = src[...]
+    vm = pl.BlockSpec(memory_space=pltpu.VMEM)
+    return pl.pallas_call(kernel, out_shape=tuple(jax.ShapeDtypeStruct(a.shape, a.dtype) for a in arrays),
+                          in_specs=[vm] * len(arrays), out_specs=(vm,) * len(arrays))(*arrays)
 
 
 def solution(mesh):
@@ -368,9 +395,7 @@
         n_keys, heads, _ = k_cache.shape
         positions = n_keys * cp_size + lax.axis_index('cp') * rows + jnp.arange(rows)
         cos_tab, sin_tab = rope_tables(positions)
-        wide_row = lambda v: v.astype(F32)[None, :]
-        out, k_new, v_new = attention_block(x_rows, wide_row(ln_gain), wide_row(q_gain), wide_row(k_gain), cos_tab, sin_tab,
-                                            w_q, w_k, w_v, w_o, k_cache, v_cache)
+        out, k_new, v_new = pass_on(*attention_block(x_rows, ln_gain, q_gain, k_gain, cos_tab, sin_tab, w_q, w_k, w_v, w_o, k_cache, v_cache))
         return out, k_new.reshape(rows, heads, HEAD_DIM), v_new.reshape(rows, heads, HEAD_DIM)
 
     return jax.shard_map(device_step, mesh=mesh, in_specs=(row_spec, cache_spec, cache_spec, whole, whole, whole, whole, whole, whole, whole), out_specs=(row_spec, cache_spec, cache_spec), check_vma=False)

time: 83.2 us -> 70.5 us (0.85)
  local copies, waits for them, and re-layouts: 5.22 us -> 0 us
  Pallas kernels: 73.2 us -> 68.5 us
  other arithmetic: 3.62 us -> 0.98 us
    pallas_call x1, Pallas kernels: 73.2 us -> 66.4 us  [attention_block(): pl.pallas_call(functools.partial(block_kernel, n_keys, heads), out_shape=...]
    unnamed x3 -> x0, local copies, waits for them, and re-layouts: 5.22 us -> none
    broadcast_in_dim x2 -> x0, other arithmetic: 2.55 us -> none  [device_step(): wide_row = lambda v: v.astype(F32)[None, :]]
    pallas_call x0 -> x1, Pallas kernels: none -> 2.17 us  [pass_on(): pl.pallas_call(kernel, out_shape=tuple((jax.ShapeDtypeStruct(a.shape, a.d...]
    sin x0 -> x1, other arithmetic: none -> 0.97 us  [rope_tables(): return (jnp.cos(angles), jnp.sin(angles))]
where the time goes in v3:
time: 70.5 us; the launch traced here: 70.2 us
  Pallas kernels  68.5 us (97%)
  other arithmetic  0.98 us (1%)
    pallas_call x1, Pallas kernels, attention_block(): pl.pallas_call(functools.partial(block_kernel, n_keys, heads), out_shape=...  66.4 us
    pallas_call x1, Pallas kernels, pass_on(): pl.pallas_call(kernel, out_shape=tuple((jax.ShapeDtypeStruct(a.shape, a.d...  2.17 us

profile of v3, /device:TPU:0, one launch (start us, length us, event | category | flops | bytes accessed | tf_op | source)
XLA Modules:
  0.0 70.2 jit_solution(4620376750710789766)
XLA Ops:
  0.7 1.0 %multiply_sine_fusion = (f32[128,64]{1,0:T(8,128)}, f32[128,64]{1,0:T(8,128)}) fusion(f32[64]{0:T(128)S(1)} %multiply_power_fusion, f32[128]{0:T(128)S(1)} %add_convert_fusion), kind=kLoop, calls=%fused_computation | loop fusion | flops 8192 | bytes 66304 | tf_op jit(solution)/shard_map/sin | solution.py:28
  1.6 66.4 %shard_map.121 = (bf16[128,2048]{1,0:T(8,128)(2,1)}, bf16[1024,128]{1,0:T(8,128)(2,1)}, bf16[1024,128]{1,0:T(8,128)(2,1)}) custom-call(bf16[128,2048]{1,0:T(8,128)(2,1)} %x_ref.1, bf16[2048]{0:T(1024)(128)(2,1)} %ln_gain.1, bf16[128]{0:T(256)(128)(2,1)} %q_gain.1, bf16[128]{0:T(256)(128)(2,1)} %k_gain.1, f32[128,64]{1,0:T(8,128)} %get-tuple-element.16.cos_tab, ...), custom_call_target="tpu_custom_call" | custom-call | tf_op jit(solution)/shard_map/pallas_call | solution.py:352
  68.0 2.2 %shard_map.122 = (bf16[128,2048]{1,0:T(8,128)(2,1)}, bf16[1024,128]{1,0:T(8,128)(2,1)}, bf16[1024,128]{1,0:T(8,128)(2,1)}) custom-call(bf16[128,2048]{1,0:T(8,128)(2,1)} %get-tuple-element.9.refs_0_, bf16[1024,128]{1,0:T(8,128)(2,1)} %get-tuple-element.10.refs_1_, bf16[1024,128]{1,0:T(8,128)(2,1)} %get-tuple-element.11.refs_2_), custom_call_target="tpu_custom_call" | custom-call | tf_op jit(solution)/shard_map/pallas_call | solution.py:383
  (2 shorter events, 0.0 us)

commit v4 on v3

--- a/solution.py
+++ b/solution.py
@@ -18,6 +18,8 @@
 KEY_TILE = 256
 PREP = 256
 GROUP = 16
+WSLOTS = 4
+CSLOTS = 4
 LEAD = 1
 
 
@@ -51,14 +53,12 @@
         n = PREP * heads
         return pltpu.make_async_copy(src.at[pl.ds(pl.multiple_of(i * n, n), n), :], raw.at[which, slot], copy_sem.at[which, slot])
 
-    WSLOTS = 4
-
     def weight_copy(w, c, slot):
         return pltpu.make_async_copy(w.at[:, pl.ds(pl.multiple_of(c * 256, 256), 256)], wbuf.at[slot], w_sem.at[slot])
 
     for c in range(WSLOTS):
         weight_copy(w_q, c, c).start()
-    for s in range(2):
+    for s in range(CSLOTS):
         cache_copy(s, 0, s).start()
         cache_copy(s, 1, s).start()
 
@@ -81,7 +81,7 @@
         return remote(qs.at[2, g], qs.at[3, g], q_send.at[2, g], q_sem.at[2, g], sibling)
 
     def prep(i):
-        slot = lax.rem(i, 2)
+        slot = lax.rem(i, CSLOTS)
         row = pl.ds(pl.multiple_of(i * PREP, PREP), PREP)
         wide[0] = raw[0, slot].astype(F32)
         for h in range(heads):
@@ -100,7 +100,7 @@
 
     def load_step(i, post):
         wslot = lax.rem(i, WSLOTS)
-        slot = lax.rem(i, 2)
+        slot = lax.rem(i, CSLOTS)
         weight_copy(w_q, 0, wslot).wait()
         cache_copy(i, 0, slot).wait()
         cache_copy(i, 1, slot).wait()
@@ -114,10 +114,10 @@
             @pl.when((ahead >= lo) & (ahead < hi))
             def _():
                 weight_copy(w, ahead - lo, wslot).start()
-        @pl.when(i + 2 < n_keys // PREP)
+        @pl.when(i + CSLOTS < n_keys // PREP)
         def _():
-            cache_copy(i + 2, 0, slot).start()
-            cache_copy(i + 2, 1, slot).start()
+            cache_copy(i + CSLOTS, 0, slot).start()
+            cache_copy(i + CSLOTS, 1, slot).start()
 
     def halves(vals):
         return [vals[:, j * 128:(j + 1) * 128] for j in range(2)]
@@ -356,7 +356,7 @@
         in_specs=[vm] * 6 + [hbm] * 6,
         out_specs=(vm, vm, vm),
         scratch_shapes=[
-            pltpu.VMEM((rows, width), BF16), pltpu.VMEM((4, width, 256), BF16),
+            pltpu.VMEM((rows, width), BF16), pltpu.VMEM((WSLOTS, width, 256), BF16),
             pltpu.VMEM((rows, 256), F32), pltpu.VMEM((rows, 128), F32), pltpu.VMEM((rows, 128), F32), pltpu.VMEM((rows, w_o.shape[0]), BF16),
             pltpu.VMEM((heads, rows, 128), BF16), pltpu.VMEM((heads, 128, rows), BF16),
             pltpu.VMEM((heads, n_keys, 128), BF16), pltpu.VMEM((heads, 128, n_keys), BF16),
@@ -366,8 +366,8 @@
             pltpu.VMEM((4, heads, 128, 256), BF16),
             pltpu.VMEM((2, heads, 2, 136, 256), F32), pltpu.VMEM((2, heads, 136, 256), F32),
             pltpu.VMEM((heads, 136, 256), F32), pltpu.VMEM((heads, 136, 256), F32),
-            pltpu.VMEM((2, 2, PREP * heads, 128), BF16), pltpu.VMEM((2, PREP * heads, 128), F32),
-            dma((2, 2)), dma((4,)), dma((3, heads)), dma((3, heads)), dma((2, heads)), dma((2, heads)), dma((heads,)), dma((heads,)),
+            pltpu.VMEM((2, CSLOTS, PREP * heads, 128), BF16), pltpu.VMEM((2, PREP * heads, 128), F32),
+            dma((2, CSLOTS)), dma((WSLOTS,)), dma((3, heads)), dma((3, heads)), dma((2, heads)), dma((2, heads)), dma((heads,)), dma((heads,)),
         ],
         compiler_params=pltpu.CompilerParams(vmem_limit_bytes=62 * 2**20, collective_id=0, has_side_effects=True),
     )(x, ln_gain, q_gain, k_gain, cos_tab, sin_tab, w_q, w_k, w_v, w_o,

time: 70.5 us -> 65.4 us (0.928)
  Pallas kernels: 68.5 us -> 63.6 us
    pallas_call x1, Pallas kernels: 66.4 us -> 61.5 us  [attention_block(): pl.pallas_call(functools.partial(block_kernel, n_keys, heads), out_shape=...]
where the time goes in v4:
time: 65.4 us; the launch traced here: 65.3 us
  Pallas kernels  63.6 us (97%)
  other arithmetic  0.98 us (1%)
    pallas_call x1, Pallas kernels, attention_block(): pl.pallas_call(functools.partial(block_kernel, n_keys, heads), out_shape=...  61.5 us
    pallas_call x1, Pallas kernels, pass_on(): pl.pallas_call(kernel, out_shape=tuple((jax.ShapeDtypeStruct(a.shape, a.d...  2.17 us

profile of v4, /device:TPU:0, one launch (start us, length us, event | category | flops | bytes accessed | tf_op | source)
XLA Modules:
  0.0 65.3 jit_solution(1357036292154621740)
XLA Ops:
  0.7 1.0 %multiply_sine_fusion = (f32[128,64]{1,0:T(8,128)}, f32[128,64]{1,0:T(8,128)}) fusion(f32[64]{0:T(128)S(1)} %multiply_power_fusion, f32[128]{0:T(128)S(1)} %add_convert_fusion), kind=kLoop, calls=%fused_computation | loop fusion | flops 8192 | bytes 66304 | tf_op jit(solution)/shard_map/sin | solution.py:30
  1.6 61.5 %shard_map.121 = (bf16[128,2048]{1,0:T(8,128)(2,1)}, bf16[1024,128]{1,0:T(8,128)(2,1)}, bf16[1024,128]{1,0:T(8,128)(2,1)}) custom-call(bf16[128,2048]{1,0:T(8,128)(2,1)} %x_ref.1, bf16[2048]{0:T(1024)(128)(2,1)} %ln_gain.1, bf16[128]{0:T(256)(128)(2,1)} %q_gain.1, bf16[128]{0:T(256)(128)(2,1)} %k_gain.1, f32[128,64]{1,0:T(8,128)} %get-tuple-element.16.cos_tab, ...), custom_call_target="tpu_custom_call" | custom-call | tf_op jit(solution)/shard_map/pallas_call | solution.py:352
  63.1 2.2 %shard_map.122 = (bf16[128,2048]{1,0:T(8,128)(2,1)}, bf16[1024,128]{1,0:T(8,128)(2,1)}, bf16[1024,128]{1,0:T(8,128)(2,1)}) custom-call(bf16[128,2048]{1,0:T(8,128)(2,1)} %get-tuple-element.9.refs_0_, bf16[1024,128]{1,0:T(8,128)(2,1)} %get-tuple-element.10.refs_1_, bf16[1024,128]{1,0:T(8,128)(2,1)} %get-tuple-element.11.refs_2_), custom_call_target="tpu_custom_call" | custom-call | tf_op jit(solution)/shard_map/pallas_call | solution.py:383
  (2 shorter events, 0.0 us)
